TPU v7x, 32 devices: a whole 2x2x4 slice. The times are simulated.
32 devices in a mesh: gx: 4 (over z), gy: 2 (over y), ea: 4 (over x, core).
Axes of the slice: x: 2, y: 2, z: 4, core: 2. Of those that a mesh axis runs over, the one named last changes fastest.
Arguments:
- load_displacement: float32 [3, 16, 32, 512], P(None, 'gx', 'gy', 'ea'), may hold values from -6 to 6
- load_enriched: float32 [15, 8192], P(None, ('gx', 'gy', 'ea')), may hold values from -24 to 24
- stiffness_shift: float32 [16, 32, 512], P('gx', 'gy', 'ea'), may hold values from 2 to 8
- enriched_diag: float32 [15, 8192], P(None, ('gx', 'gy', 'ea')), may hold values from 11 to 17
- enriched_off: float32 [15, 15, 8192], P(None, None, ('gx', 'gy', 'ea')), may hold values from -0.4 to 0.4
- coupling: float32 [3, 15, 16384], P(None, None, ('gx', 'gy', 'ea')), may hold values from -0.15 to 0.15
- slot_kind: int32 [32, 4, 128], P(('gx', 'gy', 'ea')), may hold values from 0 to 2, as said below
- slot_cell: int32 [32, 4, 128], P(('gx', 'gy', 'ea')), may hold values from 0 to 8191, as said below
- slot_node: int32 [32, 4, 128], P(('gx', 'gy', 'ea')), may hold values from 0 to 255, as said below
Outputs:
- solution_displacement: float32 [3, 16, 32, 512], P(None, 'gx', 'gy', 'ea')
- residual_displacement: float32 [3, 16, 32, 512], P(None, 'gx', 'gy', 'ea')
- solution_enriched: float32 [15, 8192], P(None, ('gx', 'gy', 'ea'))
- residual_enriched: float32 [15, 8192], P(None, ('gx', 'gy', 'ea'))
Inputs may be any that keep to these rules, and one draw needn't show every extreme that they name: `slot_kind`: within each block of 128 slots of one device to one owner the slots of kind 1 or 2 come first; in every draw some owner receives 128 such slots from each of the 4 devices of its column. `slot_cell`: distinct within one device. `slot_node`: distinct within each block of 128 slots of one device to one owner.
All inputs are finite; a program needn't handle non-finite values.
Results may differ from a plain program's by a relative error of at most 0.0003.
Values sent between devices are 32-bit elements; how exact they have to be, the bound alone decides.
A program may use at most 64 MiB of HBM per device.

v0:
```python
import functools

import jax
import jax.numpy as jnp
from jax import lax
from jax.experimental import pallas as pl
from jax.experimental.pallas import tpu as pltpu
from jax.sharding import PartitionSpec as P

ITERS = 3
CENTRE = 11.5
AXES = ("gx", "gy", "ea")
MESH = pl.DeviceIdType.MESH
F32 = jnp.float32
BF16 = jnp.bfloat16


def pieces(x):
    high = x.astype(BF16)
    return high, (x - high.astype(F32)).astype(BF16)


def stacked(x):
    high, low = pieces(x)
    return jnp.concatenate([high, low], axis=0)


def folded(product):
    half = product.shape[0] // 2
    return product[:half] + product[half:]


def iota(shape, dim):
    return lax.broadcasted_iota(jnp.int32, shape, dim)


def cg_coefficients(moment):
    def inner(first, second):
        total = None
        for i, a in enumerate(first):
            for j, b in enumerate(second):
                term = a * b * moment[i + j]
                total = term if total is None else total + term
        return total

    one = jnp.ones_like(moment[0])
    residual, direction, solution = [one], [one], []
    norm = moment[0]
    for step in range(ITERS):
        image = [CENTRE * d for d in direction] + [0.0 * one]
        for i, d in enumerate(direction):
            image[i + 1] = image[i + 1] + d
        alpha = norm / inner(direction, image)
        solution = [
            (solution[i] if i < len(solution) else 0.0) + alpha * d
            for i, d in enumerate(direction)
        ]
        residual = [
            (residual[i] if i < len(residual) else 0.0) - alpha * d for i, d in enumerate(image)
        ]
        if step + 1 < ITERS:
            new = inner(residual, residual)
            ratio = new / norm
            norm = new
            direction = [
                r + (ratio * direction[i] if i < len(direction) else 0.0)
                for i, r in enumerate(residual)
            ]
    return solution, residual


def kernel(
    sizes, groups,
    load_v, load_w, shift_h, diag_h, off_h, coupling_h, kind_h, cell_h, node_h,
    vu, wu, coefs,
    w_first, shift, diag, off, coupling, kind, cell, node, load_s,
    weights, stiff, lanes, lanes_t, rows, rows_b, nodes_mine, nodes_recv, centre_diag,
    node_in, x_in, y_in, z_in, w_in, t_in, y_out, z_out, t_out, red, red_out,
    node_s, node_r, x_s, x_r, y_s, y_r, z_s, z_r, w_s, w_r, t_s, t_r, red_s, red_r,
):
    n_gx, n_gy, n_ea = sizes
    comps, dx, dy, dz = load_v.shape
    ecomp, enb = load_w.shape
    epad = wu.shape[1]
    cap = node.shape[2]
    per = dx * dy
    allrows = comps * per
    groups8 = allrows // 8
    gi, gj, ek = (lax.axis_index(a) for a in AXES)
    own = {"gx": gi, "gy": gj, "ea": ek}
    count = dict(zip(AXES, sizes))

    def members(group):
        total = 1
        for a in group:
            total *= count[a]
        me = 0
        for a in group:
            me = me * count[a] + own[a]

        def target(d):
            flat = lax.rem(me + d, total)
            coords = dict(own)
            for a in reversed(group):
                coords[a] = lax.rem(flat, count[a])
                flat = lax.div(flat, count[a])
            return tuple(coords[a] for a in AXES)

        return total, me, target

    barrier = pltpu.get_barrier_semaphore()
    expected = 0
    for group in groups:
        total, _, target = members(group)
        for d in range(1, total):
            pl.semaphore_signal(barrier, inc=1, device_id=target(d), device_id_type=MESH)
        expected += total - 1

    loads = {}
    for at, (name, src, dst) in enumerate((
        ("cell", cell_h, cell), ("v", load_v, vu.at[0]), ("node", node_h, node),
        ("kind", kind_h, kind), ("w", load_w, w_first), ("coupling", coupling_h, coupling),
        ("shift", shift_h, shift), ("off", off_h, off), ("diag", diag_h, diag),
    )):
        loads[name] = pltpu.make_async_copy(src, dst, load_s.at[at])
        loads[name].start()

    def columns(tile):
        full = jnp.concatenate(
            [tile.astype(F32), jnp.zeros((cap - tile.shape[0], cap), F32)], axis=0
        )
        return jnp.transpose(full).astype(jnp.int32)

    loads["cell"].wait()
    tile = cell[0]
    tile_row = lax.div(tile, dz)
    tile_lane = tile - tile_row * dz
    lane_columns = columns(tile_lane)
    for o in range(n_ea):
        span = slice(o * cap, (o + 1) * cap)
        lanes[:, span] = jnp.where(
            iota((dz, cap), 0) == tile_lane[o : o + 1], 1.0, 0.0
        ).astype(BF16)
        lanes_t[span, :] = jnp.where(
            iota((cap, dz), 1) == lane_columns[:, o : o + 1], 1.0, 0.0
        ).astype(BF16)
        r = jnp.where(iota((per, cap), 0) == tile_row[o : o + 1], 1.0, 0.0)
        rows[:, span] = r
        rows_b[:, span] = r.astype(BF16)
    loads["node"].wait()
    for o in range(n_ea):
        nodes_mine[o] = jnp.where(
            iota((enb, cap), 0) == node[0, o : o + 1, :], 1.0, 0.0
        ).astype(BF16)
    loads["kind"].wait()
    loads["coupling"].wait()
    no_row = jnp.zeros((epad - ecomp, n_ea * cap), F32)
    for i in range(comps):
        for o in range(n_ea):
            k = kind[0, o : o + 1, :]
            heavi = jnp.where(k >= 1, 1.0, 0.0)
            tip = jnp.where(k == 2, 1.0, 0.0)
            mask = jnp.where(iota((ecomp, cap), 0) < 3, heavi, tip)
            span = slice(o * cap, (o + 1) * cap)
            weights[i, :, span] = jnp.concatenate(
                [coupling[i, :, span] * mask, no_row[:, span]], axis=0
            )
    loads["w"].wait()
    wu[0] = jnp.concatenate([w_first[...], jnp.zeros((epad - ecomp, enb), F32)], axis=0)
    loads["v"].wait()

    pl.semaphore_wait(barrier, expected)

    def partner(d):
        return lax.rem(ek + d, n_ea)

    has = {
        ("gx", 1): gi < n_gx - 1, ("gx", -1): gi > 0,
        ("gy", 1): gj < n_gy - 1, ("gy", -1): gj > 0,
        ("ea", 1): ek < n_ea - 1, ("ea", -1): ek > 0,
    }
    beside = {
        ("gx", s): (gi + s, gj, ek) for s in (1, -1)
    } | {("gy", s): (gi, gj + s, ek) for s in (1, -1)} | {
        ("ea", s): (gi, gj, ek + s) for s in (1, -1)
    }
    slot = {1: 0, -1: 1}

    def remote(src, dst, s_sem, r_sem, device):
        return pltpu.make_async_remote_copy(
            src_ref=src, dst_ref=dst, send_sem=s_sem, recv_sem=r_sem,
            device_id=device, device_id_type=MESH,
        )

    def x_copy(op, s):
        return remote(
            vu.at[op, :, dx - 1 if s == 1 else 0], x_in.at[op, slot[s]],
            x_s.at[op, slot[s]], x_r.at[op, slot[s]], beside["gx", s],
        )

    def y_copy(op, s):
        return remote(
            y_out.at[op, slot[s]], y_in.at[op, slot[s]],
            y_s.at[op, slot[s]], y_r.at[op, slot[s]], beside["gy", s],
        )

    def z_copy(op, s):
        return remote(
            z_out.at[op, slot[s]], z_in.at[op, slot[s]],
            z_s.at[op, slot[s]], z_r.at[op, slot[s]], beside["ea", s],
        )

    def w_copy(op, d):
        return remote(
            wu.at[op], w_in.at[op, ek], w_s.at[op, d], w_r.at[op, d], (gi, gj, partner(d))
        )

    def t_copy(op, d):
        return remote(
            t_out.at[op, partner(d)], t_in.at[op, ek], t_s.at[op, d], t_r.at[op, d],
            (gi, gj, partner(d)),
        )

    def node_copy(d):
        return remote(
            node, node_in.at[ek], node_s.at[d], node_r.at[d], (gi, gj, partner(d))
        )

    lane_i = iota((8, dz), 1)
    lane_r = iota((1, dz), 1)

    def product(op_a, op_b):
        pv = jnp.sum((vu[op_a] * vu[op_b]).reshape(groups8, 8, dz), axis=0)
        pw = jnp.sum(wu[op_a] * wu[op_b], axis=0, keepdims=True)
        row = jnp.sum(pv, axis=0, keepdims=True)
        total = row
        for b in range(enb // dz):
            total = total + pw[:, b * dz : (b + 1) * dz]
        return total

    moments = []
    for op in range(ITERS):
        for s in (1, -1):
            @pl.when(has["gx", s])
            def _():
                x_copy(op, s).start()
        for d in range(1, n_ea):
            w_copy(op, d).start()
            if op == 0:
                node_copy(d).start()
        v2 = vu[op].reshape(allrows, dz)
        for i in range(comps):
            for a in range(dx):
                at = i * dx + a
                y_out[op, 0, at : at + 1, :] = vu[op, i, a, dy - 1 : dy, :]
                y_out[op, 1, at : at + 1, :] = vu[op, i, a, 0:1, :]
        for s in (1, -1):
            @pl.when(has["gy", s])
            def _():
                y_copy(op, s).start()
        up = jnp.zeros((8, dz), F32)
        down = jnp.zeros((8, dz), F32)
        for g in range(groups8):
            part = v2[8 * g : 8 * g + 8]
            up = jnp.where(lane_i == g, part[:, dz - 1 : dz], up)
            down = jnp.where(lane_i == g, part[:, 0:1], down)
        z_out[op, 0] = up
        z_out[op, 1] = down
        for s in (1, -1):
            @pl.when(has["ea", s])
            def _():
                z_copy(op, s).start()
        seen = folded(jnp.dot(stacked(v2), lanes[...], preferred_element_type=F32))
        total = None
        for i in range(comps):
            picked = jnp.sum(seen[i * per : (i + 1) * per] * rows[...], axis=0, keepdims=True)
            term = weights[i] * picked
            total = term if total is None else total + term
        for o in range(n_ea):
            t_out[op, o] = total[:, o * cap : (o + 1) * cap]
        for d in range(1, n_ea):
            t_copy(op, d).start()

        if op == 0:
            loads["off"].wait()
            loads["diag"].wait()
            for p in range(ecomp):
                whole = 0.5 * (off[p] + off[:, p, :])
                whole = jnp.where(
                    iota((ecomp, enb), 0) == p, diag[p : p + 1, :] - CENTRE, whole
                )
                stiff[p] = jnp.concatenate(
                    [whole, jnp.zeros((epad - ecomp, enb), F32)], axis=0
                )
            loads["shift"].wait()
            centre_diag[...] = shift[...] + (6.0 - CENTRE)
            node_in[ek] = node[...]
        v4 = vu[op]
        zero = jnp.zeros((comps, 1, dy, dz), F32)
        near = jnp.concatenate([zero, v4[:, : dx - 1]], axis=1) + jnp.concatenate(
            [v4[:, 1:], zero], axis=1
        )
        near = near.reshape(allrows, dz)
        lane_all = iota((allrows, dz), 1)
        row_all = lax.rem(iota((allrows, dz), 0), dy)
        near = near + jnp.where(lane_all == 0, 0.0, pltpu.roll(v2, 1, 1))
        near = near + jnp.where(lane_all == dz - 1, 0.0, pltpu.roll(v2, dz - 1, 1))
        near = near + jnp.where(row_all == 0, 0.0, pltpu.roll(v2, 1, 0))
        near = near + jnp.where(row_all == dy - 1, 0.0, pltpu.roll(v2, allrows - 1, 0))
        vu[op + 1] = centre_diag[...][None] * v4 - near.reshape(v4.shape)
        w = wu[op]
        acc = stiff[0] * w[0:1]
        for p in range(1, ecomp):
            acc = acc + stiff[p] * w[p : p + 1]
        if op == 0:
            moments.append(product(0, 0))
        else:
            moments.append(product(op, op))

        w_in[op, ek] = w
        t_in[op, ek] = t_out[op, ek]
        if op + 1 == ITERS:
            packed = jnp.zeros((1, dz), F32)
            for n, row in enumerate(moments):
                packed = jnp.where(lane_r == n, jnp.sum(row, axis=1, keepdims=True), packed)
        if op == 0:
            for d in range(1, n_ea):
                node_copy(d).wait_recv()
            own_rows = jnp.concatenate(
                [node_in[o, 0, pl.ds(ek, 1), :] for o in range(n_ea)], axis=0
            )
            node_columns = columns(own_rows)
            for o in range(n_ea):
                nodes_recv[o * cap : (o + 1) * cap, :] = jnp.where(
                    iota((cap, enb), 1) == node_columns[:, o : o + 1], 1.0, 0.0
                ).astype(BF16)
        for d in range(1, n_ea):
            w_copy(op, d).wait_recv()
        values = jnp.concatenate(
            [
                folded(jnp.dot(stacked(w_in[op, o]), nodes_mine[o], preferred_element_type=F32))
                for o in range(n_ea)
            ],
            axis=1,
        )
        spread_h, spread_l = [], []
        for i in range(comps):
            h, l = pieces(jnp.sum(weights[i] * values, axis=0, keepdims=True))
            spread_h.append(rows_b[...] * h)
            spread_l.append(rows_b[...] * l)
        added = folded(
            jnp.dot(
                jnp.concatenate(spread_h + spread_l, axis=0), lanes_t[...],
                preferred_element_type=F32,
            )
        )
        vu[op + 1] += added.reshape(comps, dx, dy, dz)
        for s in (1, -1):
            @pl.when(has["gx", -s])
            def _():
                x_copy(op, s).wait_recv()
                edge = 0 if s == 1 else dx - 1
                vu[op + 1, :, edge] -= x_in[op, slot[s]]

            @pl.when(has["gy", -s])
            def _():
                y_copy(op, s).wait_recv()
                edge = 0 if s == 1 else dy - 1
                for i in range(comps):
                    for a in range(dx):
                        at = i * dx + a
                        vu[op + 1, i, a, edge : edge + 1, :] -= y_in[op, slot[s], at : at + 1, :]

            @pl.when(has["ea", -s])
            def _():
                z_copy(op, s).wait_recv()
                edge = 0 if s == 1 else dz - 1
                tile = z_in[op, slot[s]]
                for i in range(comps):
                    for a in range(dx):
                        for b in range(dy // 8):
                            g = (i * dx + a) * (dy // 8) + b
                            vu[op + 1, i, a, 8 * b : 8 * b + 8, :] -= jnp.where(
                                lane_i == edge, tile[:, g : g + 1], 0.0
                            )
        for d in range(1, n_ea):
            t_copy(op, d).wait_recv()
        terms = jnp.concatenate([t_in[op, o] for o in range(n_ea)], axis=1)
        acc = acc + folded(
            jnp.dot(stacked(terms), nodes_recv[...], preferred_element_type=F32)
        )
        wu[op + 1] = acc
        moments.append(product(op, op + 1))

    last = 2 * ITERS - 1
    packed = jnp.where(lane_r == last, jnp.sum(moments[last], axis=1, keepdims=True), packed)
    for stage, group in enumerate(groups):
        total, me, target = members(group)
        red_out[stage] = packed

        def red_copy(d):
            return remote(
                red_out.at[stage], red.at[stage, me], red_s.at[stage, d], red_r.at[stage, d],
                target(d),
            )

        for d in range(1, total):
            red_copy(d).start()
        red[stage, me] = packed
        for d in range(1, total):
            red_copy(d).wait_recv()
        packed = jnp.sum(red[stage, :total], axis=0)

    sol, res = cg_coefficients([packed[:, n : n + 1] for n in range(2 * ITERS)])
    tile = jnp.zeros((1, dz), F32)
    for n, c in enumerate(sol + res):
        tile = jnp.where(lane_r == n, c, tile)
    coefs[...] = tile

    for op in range(ITERS):
        for s in (1, -1):
            @pl.when(has["gx", s])
            def _():
                x_copy(op, s).wait_send()

            @pl.when(has["gy", s])
            def _():
                y_copy(op, s).wait_send()

            @pl.when(has["ea", s])
            def _():
                z_copy(op, s).wait_send()
        for d in range(1, n_ea):
            w_copy(op, d).wait_send()
            t_copy(op, d).wait_send()
            if op == 0:
                node_copy(d).wait_send()
    for stage, group in enumerate(groups):
        total, me, target = members(group)
        for d in range(1, total):
            remote(
                red_out.at[stage], red.at[stage, me], red_s.at[stage, d], red_r.at[stage, d],
                target(d),
            ).wait_send()


def combine_kernel(vu, wu, coefs, sol_v, res_v, sol_w, res_w):
    ecomp = sol_w.shape[0]
    tile = coefs[...]
    solution = [tile[:, n : n + 1] for n in range(ITERS)]
    residual = [tile[:, ITERS + n : ITERS + n + 1] for n in range(ITERS + 1)]

    def combine(factors, terms):
        out = factors[0] * terms[0]
        for f, t in zip(factors[1:], terms[1:]):
            out = out + f * t
        return out

    shape = sol_v.shape
    flat = (shape[0] * shape[1] * shape[2], shape[3])
    v_terms = [vu[n].reshape(flat) for n in range(ITERS + 1)]
    w_terms = [wu[n] for n in range(ITERS + 1)]
    sol_v[...] = combine(solution, v_terms).reshape(shape)
    res_v[...] = combine(residual, v_terms).reshape(shape)
    sol_w[...] = combine(solution, w_terms)[:ecomp]
    res_w[...] = combine(residual, w_terms)[:ecomp]


def body(sizes, *args):
    load_v, load_w, shift, diag, off, coupling, kind, cell, node = args
    n_ea = sizes[2]
    total = sizes[0] * sizes[1] * sizes[2]
    groups = (AXES,) if total <= 64 else (("gx",), ("gy", "ea"))
    widest = total if total <= 64 else max(sizes[0], sizes[1] * sizes[2])
    comps, dx, dy, dz = load_v.shape
    ecomp, enb = load_w.shape
    cap = node.shape[2]
    vmem = pltpu.VMEM
    dma = pltpu.SemaphoreType.DMA
    y_rows = -(-comps * dx // 8) * 8
    epad = -(-ecomp // 16) * 16
    slots = n_ea * cap
    scratch = [
        vmem(load_w.shape, F32), vmem(shift.shape, F32), vmem(diag.shape, F32),
        vmem(off.shape, F32), vmem(coupling.shape, F32),
        vmem(kind.shape, jnp.int32), vmem(cell.shape, jnp.int32), vmem(node.shape, jnp.int32),
        dma((9,)),
        vmem((comps, epad, slots), F32),
        vmem((ecomp, epad, enb), F32),
        vmem((dz, slots), BF16),
        vmem((slots, dz), BF16),
        vmem((dx * dy, slots), F32),
        vmem((dx * dy, slots), BF16),
        vmem((n_ea, enb, cap), BF16),
        vmem((slots, enb), BF16),
        vmem((dx, dy, dz), F32),
        vmem((n_ea,) + node.shape, jnp.int32),
        vmem((ITERS, 2, comps, dy, dz), F32),
        vmem((ITERS, 2, y_rows, dz), F32),
        vmem((ITERS, 2, 8, dz), F32),
        vmem((ITERS, n_ea, epad, enb), F32),
        vmem((ITERS, n_ea, epad, cap), F32),
        vmem((ITERS, 2, y_rows, dz), F32),
        vmem((ITERS, 2, 8, dz), F32),
        vmem((ITERS, n_ea, epad, cap), F32),
        vmem((len(groups), widest, 1, dz), F32),
        vmem((len(groups), 1, dz), F32),
        dma((n_ea,)), dma((n_ea,)),
        dma((ITERS, 2)), dma((ITERS, 2)),
        dma((ITERS, 2)), dma((ITERS, 2)),
        dma((ITERS, 2)), dma((ITERS, 2)),
        dma((ITERS, n_ea)), dma((ITERS, n_ea)),
        dma((ITERS, n_ea)), dma((ITERS, n_ea)),
        dma((len(groups), widest)), dma((len(groups), widest)),
    ]
    basis = pl.pallas_call(
        functools.partial(kernel, sizes, groups),
        out_shape=(
            pltpu.VMEM((ITERS + 1,) + load_v.shape, F32),
            pltpu.VMEM((ITERS + 1, epad, enb), F32),
            pltpu.VMEM((1, dz), F32),
        ),
        in_specs=[pl.BlockSpec(memory_space=pltpu.HBM)] * 9,
        out_specs=[pl.BlockSpec(memory_space=vmem)] * 3,
        scratch_shapes=scratch,
        compiler_params=pltpu.CompilerParams(
            collective_id=0, has_side_effects=True
        ),
        name="krylov",
    )(*args)
    return tuple(
        pl.pallas_call(
            combine_kernel,
            out_shape=tuple(
                jax.ShapeDtypeStruct(like.shape, F32)
                for like in (load_v, load_v, load_w, load_w)
            ),
            in_specs=[pl.BlockSpec(memory_space=vmem)] * 3,
            out_specs=[pl.BlockSpec(memory_space=vmem)] * 4,
            compiler_params=pltpu.CompilerParams(vmem_limit_bytes=8 << 20),
            name="combine",
        )(*basis)
    )


def solution(mesh):
    column = ("gx", "gy", "ea")
    placed = (
        P(None, "gx", "gy", "ea"),
        P(None, column),
        P("gx", "gy", "ea"),
        P(None, column),
        P(None, None, column),
        P(None, None, column),
        P(column, None, None),
        P(column, None, None),
        P(column, None, None),
    )
    return jax.shard_map(
        functools.partial(body, tuple(mesh.shape[a] for a in AXES)),
        mesh=mesh,
        in_specs=placed,
        out_specs=(
            P(None, "gx", "gy", "ea"),
            P(None, "gx", "gy", "ea"),
            P(None, column),
            P(None, column),
        ),
        check_vma=False,
    )
```

profile of v0, /device:TPU:0, one launch (start us, length us, event | category | flops | bytes accessed | tf_op | source)
XLA Modules:
  0.0 24.5 jit_solution(11840547472090305423)
XLA Ops:
  0.6 23.0 %krylov.1 = (f32[4,3,4,16,128]{4,3,2,1,0:T(8,128)S(1)}, f32[4,16,256]{2,1,0:T(8,128)S(1)}, f32[1,128]{1,0:T(1,128)S(1)}) custom-call(f32[3,4,16,128]{3,2,1,0:T(8,128)} %load_v.1, f32[15,256]{1,0:T(8,128)} %load_w.1, f32[4,16,128]{2,1,0:T(8,128)} %shift_h.1, f32[15,256]{1,0:T(8,128)} %diag_h.1, f32[15,15,256]{2,1,0:T(8,128)} %off_h.1, ...), custom_call_target="tpu_custom_call" | custom-call | tf_op jit(solution)/shard_map/krylov/pallas_call | solution.py:516
  23.7 0.8 %combine.1 = (f32[3,4,16,128]{3,2,1,0:T(8,128)}, f32[3,4,16,128]{3,2,1,0:T(8,128)}, f32[15,256]{1,0:T(8,128)}, f32[15,256]{1,0:T(8,128)}) custom-call(f32[4,3,4,16,128]{4,3,2,1,0:T(8,128)S(1)} %get-tuple-element.7.vu, f32[4,16,256]{2,1,0:T(8,128)S(1)} %get-tuple-element.8.wu, f32[1,128]{1,0:T(1,128)S(1)} %get-tuple-element.9.coefs), custom_call_target="tpu_custom_call" | custom-call | tf_op jit(solution)/shard_map/combine/pallas_call | solution.py:532
where the time goes:
time: 24.6 us; the launch traced here: 24.5 us
  Pallas kernels  23.8 us (97%)
  between operations  0.64 us (3%)
    pallas_call x1, Pallas kernels, body(): pl.pallas_call(functools.partial(kernel, sizes, groups), out_shape=(pltpu...  23 us
    pallas_call x1, Pallas kernels, body(): pl.pallas_call(combine_kernel, out_shape=tuple((jax.ShapeDtypeStruct(like...  0.78 us

commit v1 on v0

--- a/solution.py
+++ b/solution.py
@@ -109,12 +109,21 @@
         return total, me, target
 
     barrier = pltpu.get_barrier_semaphore()
+    wide = n_gx - 1 > ITERS
     expected = 0
-    for group in groups:
+    for group in groups if wide else (("gy", "ea"),):
         total, _, target = members(group)
         for d in range(1, total):
             pl.semaphore_signal(barrier, inc=1, device_id=target(d), device_id_type=MESH)
         expected += total - 1
+    if not wide:
+        for s, there in ((1, gi < n_gx - 1), (-1, gi > 0)):
+            @pl.when(there)
+            def _():
+                pl.semaphore_signal(
+                    barrier, inc=1, device_id=(gi + s, gj, ek), device_id_type=MESH
+                )
+            expected = expected + jnp.where(there, 1, 0)
 
     loads = {}
     for at, (name, src, dst) in enumerate((

time: 24.6 us -> 24.2 us (0.984)
  Pallas kernels: 23.8 us -> 23.4 us
    pallas_call x1, Pallas kernels: 23 us -> 22.6 us  [body(): pl.pallas_call(functools.partial(kernel, sizes, groups), out_shape=(pltpu...]
where the time goes in v1:
time: 24.2 us; the launch traced here: 24 us
  Pallas kernels  23.4 us (97%)
  between operations  0.64 us (3%)
    pallas_call x1, Pallas kernels, body(): pl.pallas_call(functools.partial(kernel, sizes, groups), out_shape=(pltpu...  22.6 us
    pallas_call x1, Pallas kernels, body(): pl.pallas_call(combine_kernel, out_shape=tuple((jax.ShapeDtypeStruct(like...  0.78 us

profile of v1, /device:TPU:0, one launch (start us, length us, event | category | flops | bytes accessed | tf_op | source)
XLA Modules:
  0.0 24.0 jit_solution(11005579136934437302)
XLA Ops:
  0.6 22.6 %krylov.1 = (f32[4,3,4,16,128]{4,3,2,1,0:T(8,128)S(1)}, f32[4,16,256]{2,1,0:T(8,128)S(1)}, f32[1,128]{1,0:T(1,128)S(1)}) custom-call(f32[3,4,16,128]{3,2,1,0:T(8,128)} %load_v.1, f32[15,256]{1,0:T(8,128)} %load_w.1, f32[4,16,128]{2,1,0:T(8,128)} %shift_h.1, f32[15,256]{1,0:T(8,128)} %diag_h.1, f32[15,15,256]{2,1,0:T(8,128)} %off_h.1, ...), custom_call_target="tpu_custom_call" | custom-call | tf_op jit(solution)/shard_map/krylov/pallas_call | solution.py:525
  23.3 0.8 %combine.1 = (f32[3,4,16,128]{3,2,1,0:T(8,128)}, f32[3,4,16,128]{3,2,1,0:T(8,128)}, f32[15,256]{1,0:T(8,128)}, f32[15,256]{1,0:T(8,128)}) custom-call(f32[4,3,4,16,128]{4,3,2,1,0:T(8,128)S(1)} %get-tuple-element.7.vu, f32[4,16,256]{2,1,0:T(8,128)S(1)} %get-tuple-element.8.wu, f32[1,128]{1,0:T(1,128)S(1)} %get-tuple-element.9.coefs), custom_call_target="tpu_custom_call" | custom-call | tf_op jit(solution)/shard_map/combine/pallas_call | solution.py:541

commit v2 on v0

v2 whole, which is shorter than its diff:
```python
import functools

import jax
import jax.numpy as jnp
from jax import lax
from jax.experimental import pallas as pl
from jax.experimental.pallas import tpu as pltpu
from jax.sharding import PartitionSpec as P

ITERS = 3
CENTRE = 11.5
AXES = ("gx", "gy", "ea")
MESH = pl.DeviceIdType.MESH
F32 = jnp.float32
BF16 = jnp.bfloat16


def pieces(x):
    high = x.astype(BF16)
    return high, (x - high.astype(F32)).astype(BF16)


def stacked(x):
    high, low = pieces(x)
    return jnp.concatenate([high, low], axis=0)


def folded(product):
    half = product.shape[0] // 2
    return product[:half] + product[half:]


def iota(shape, dim):
    return lax.broadcasted_iota(jnp.int32, shape, dim)


def cg_coefficients(moment):
    def inner(first, second):
        total = None
        for i, a in enumerate(first):
            for j, b in enumerate(second):
                term = a * b * moment[i + j]
                total = term if total is None else total + term
        return total

    one = jnp.ones_like(moment[0])
    residual, direction, solution = [one], [one], []
    norm = moment[0]
    for step in range(ITERS):
        image = [CENTRE * d for d in direction] + [0.0 * one]
        for i, d in enumerate(direction):
            image[i + 1] = image[i + 1] + d
        alpha = norm / inner(direction, image)
        solution = [
            (solution[i] if i < len(solution) else 0.0) + alpha * d
            for i, d in enumerate(direction)
        ]
        residual = [
            (residual[i] if i < len(residual) else 0.0) - alpha * d for i, d in enumerate(image)
        ]
        if step + 1 < ITERS:
            new = inner(residual, residual)
            ratio = new / norm
            norm = new
            direction = [
                r + (ratio * direction[i] if i < len(direction) else 0.0)
                for i, r in enumerate(residual)
            ]
    return solution, residual


def kernel(
    sizes, groups,
    load_v, load_w, shift_h, diag_h, off_h, coupling_h, kind_h, cell_h, node_h,
    vu, wu, coefs,
    w_first, shift, diag, off, coupling, kind, cell, node, load_s,
    weights, win, stiff, lanes, lanes_t, rows, rows_b, nodes_mine, nodes_recv, nodes_t,
    centre_diag, node_in, kind_in, coup_in,
    x_in, y_in, z_in, w_in, p_in, s_in, y_out, z_out, p_out, s_out, red, red_out,
    node_s, node_r, kind_s, kind_r, coup_s, coup_r,
    x_s, x_r, y_s, y_r, z_s, z_r, w_s, w_r, p_s, p_r, s_s, s_r, red_s, red_r,
):
    n_gx, n_gy, n_ea = sizes
    comps, dx, dy, dz = load_v.shape
    ecomp, enb = load_w.shape
    epad = wu.shape[1]
    cap = node.shape[2]
    per = dx * dy
    allrows = comps * per
    groups8 = allrows // 8
    edge_rows = comps * dx
    gi, gj, ek = (lax.axis_index(a) for a in AXES)
    own = {"gx": gi, "gy": gj, "ea": ek}
    count = dict(zip(AXES, sizes))

    def members(group):
        total = 1
        for a in group:
            total *= count[a]
        me = 0
        for a in group:
            me = me * count[a] + own[a]

        def target(d):
            flat = lax.rem(me + d, total)
            coords = dict(own)
            for a in reversed(group):
                coords[a] = lax.rem(flat, count[a])
                flat = lax.div(flat, count[a])
            return tuple(coords[a] for a in AXES)

        return total, me, target

    has = {
        ("gx", 1): gi < n_gx - 1, ("gx", -1): gi > 0,
        ("gy", 1): gj < n_gy - 1, ("gy", -1): gj > 0,
        ("ea", 1): ek < n_ea - 1, ("ea", -1): ek > 0,
    }
    beside = {
        ("gx", s): (gi + s, gj, ek) for s in (1, -1)
    } | {("gy", s): (gi, gj + s, ek) for s in (1, -1)} | {
        ("ea", s): (gi, gj, ek + s) for s in (1, -1)
    }
    slot = {1: 0, -1: 1}

    barrier = pltpu.get_barrier_semaphore()
    wide = n_gx - 1 > ITERS
    expected = 0
    for group in groups if wide else (("gy", "ea"),):
        total, _, target = members(group)
        for d in range(1, total):
            pl.semaphore_signal(barrier, inc=1, device_id=target(d), device_id_type=MESH)
        expected += total - 1
    if not wide:
        for s in (1, -1):
            @pl.when(has["gx", s])
            def _():
                pl.semaphore_signal(
                    barrier, inc=1, device_id=beside["gx", s], device_id_type=MESH
                )
            expected = expected + jnp.where(has["gx", s], 1, 0)

    loads = {}
    for at, (name, src, dst) in enumerate((
        ("cell", cell_h, cell), ("v", load_v, vu.at[0]), ("w", load_w, w_first),
        ("node", node_h, node), ("kind", kind_h, kind), ("coupling", coupling_h, coupling),
        ("shift", shift_h, shift), ("off", off_h, off), ("diag", diag_h, diag),
    )):
        loads[name] = pltpu.make_async_copy(src, dst, load_s.at[at])
        loads[name].start()

    for s in (1, -1):
        for name, buffer in (("gx", x_in), ("gy", y_in), ("ea", z_in)):
            @pl.when(jnp.logical_not(has[name, -s]))
            def _():
                for op in range(ITERS):
                    buffer[op, slot[s]] = jnp.zeros(buffer.shape[2:], F32)

    def partner(d):
        return lax.rem(ek + d, n_ea)

    def remote(src, dst, s_sem, r_sem, device):
        return pltpu.make_async_remote_copy(
            src_ref=src, dst_ref=dst, send_sem=s_sem, recv_sem=r_sem,
            device_id=device, device_id_type=MESH,
        )

    def x_copy(op, s):
        return remote(
            vu.at[op, :, dx - 1 if s == 1 else 0], x_in.at[op, slot[s]],
            x_s.at[op, slot[s]], x_r.at[op, slot[s]], beside["gx", s],
        )

    def y_copy(op, s):
        return remote(
            y_out.at[op, slot[s]], y_in.at[op, slot[s]],
            y_s.at[op, slot[s]], y_r.at[op, slot[s]], beside["gy", s],
        )

    def z_copy(op, s):
        return remote(
            z_out.at[op, slot[s]], z_in.at[op, slot[s]],
            z_s.at[op, slot[s]], z_r.at[op, slot[s]], beside["ea", s],
        )

    def column_copy(src, dst, s_sem, r_sem, d):
        return remote(src, dst.at[ek], s_sem.at[d], r_sem.at[d], (gi, gj, partner(d)))

    def w_copy(d):
        return column_copy(wu.at[0], w_in, w_s, w_r, d)

    def p_copy(op, d):
        return column_copy(
            p_out.at[op, partner(d)], p_in.at[op], p_s.at[op], p_r.at[op], d
        )

    def s_copy(op, d):
        return column_copy(
            s_out.at[op, partner(d)], s_in.at[op], s_s.at[op], s_r.at[op], d
        )

    def block(d):
        return pl.ds(pl.multiple_of(partner(d) * cap, cap), cap)

    def table_copies(d):
        return (
            column_copy(node, node_in, node_s, node_r, d),
            column_copy(kind, kind_in, kind_s, kind_r, d),
            column_copy(coupling.at[:, :, block(d)], coup_in, coup_s, coup_r, d),
        )

    lane_i = iota((8, dz), 1)
    lane_r = iota((1, dz), 1)
    row_i = iota((dy, dz), 0)
    lane_b = iota((dy, dz), 1)

    def columns(tile):
        full = jnp.concatenate(
            [tile.astype(F32), jnp.zeros((cap - tile.shape[0], cap), F32)], axis=0
        )
        return jnp.transpose(full).astype(jnp.int32)

    def slabs(o):
        return slice(o * cap, (o + 1) * cap)

    def halo_pack(op):
        v2 = vu[op].reshape(allrows, dz)
        for i in range(comps):
            for a in range(dx):
                at = i * dx + a
                y_out[op, 0, at : at + 1, :] = vu[op, i, a, dy - 1 : dy, :]
                y_out[op, 1, at : at + 1, :] = vu[op, i, a, 0:1, :]
        up = jnp.zeros((8, dz), F32)
        down = jnp.zeros((8, dz), F32)
        for g in range(groups8):
            part = v2[8 * g : 8 * g + 8]
            up = jnp.where(lane_i == g, part[:, dz - 1 : dz], up)
            down = jnp.where(lane_i == g, part[:, 0:1], down)
        z_out[op, 0] = up
        z_out[op, 1] = down

    def halo_send(op):
        for s in (1, -1):
            for name, copy in (("gx", x_copy), ("gy", y_copy), ("ea", z_copy)):
                @pl.when(has[name, s])
                def _():
                    copy(op, s).start()

    def halo_wait(op):
        for s in (1, -1):
            for name, copy in (("gx", x_copy), ("gy", y_copy), ("ea", z_copy)):
                @pl.when(has[name, -s])
                def _():
                    copy(op, s).wait_recv()

    def pick(op):
        v2 = vu[op].reshape(allrows, dz)
        seen = folded(jnp.dot(stacked(v2), lanes[...], preferred_element_type=F32))
        for i in range(comps):
            picked = jnp.sum(seen[i * per : (i + 1) * per] * rows[...], axis=0, keepdims=True)
            for o in range(n_ea):
                p_out[op, o, i : i + 1, :] = picked[:, slabs(o)]

    def pick_send(op):
        for d in range(1, n_ea):
            p_copy(op, d).start()

    def local(op):
        v4 = vu[op]
        v2 = v4.reshape(allrows, dz)
        zero = jnp.zeros((comps, 1, dy, dz), F32)
        near = jnp.concatenate([zero, v4[:, : dx - 1]], axis=1) + jnp.concatenate(
            [v4[:, 1:], zero], axis=1
        )
        near = near.reshape(allrows, dz)
        lane_all = iota((allrows, dz), 1)
        row_all = lax.rem(iota((allrows, dz), 0), dy)
        near = near + jnp.where(lane_all == 0, 0.0, pltpu.roll(v2, 1, 1))
        near = near + jnp.where(lane_all == dz - 1, 0.0, pltpu.roll(v2, dz - 1, 1))
        near = near + jnp.where(row_all == 0, 0.0, pltpu.roll(v2, 1, 0))
        near = near + jnp.where(row_all == dy - 1, 0.0, pltpu.roll(v2, allrows - 1, 0))
        vu[op + 1] = centre_diag[...][None] * v4 - near.reshape(v4.shape)

    def local_nodes(op):
        w = wu[op]
        acc = stiff[0] * w[0:1]
        for p in range(1, ecomp):
            acc = acc + stiff[p] * w[p : p + 1]
        wu[op + 1] = acc

    def product(op_a, op_b):
        pv = jnp.sum((vu[op_a] * vu[op_b]).reshape(groups8, 8, dz), axis=0)
        pw = jnp.sum(wu[op_a] * wu[op_b], axis=0, keepdims=True)
        total = jnp.sum(pv, axis=0, keepdims=True)
        for b in range(enb // dz):
            total = total + pw[:, b * dz : (b + 1) * dz]
        return total

    def nodes_step(op):
        p_in[op, ek] = p_out[op, ek]
        for d in range(1, n_ea):
            p_copy(op, d).wait_recv()
        terms = []
        for o in range(n_ea):
            total = None
            for i in range(comps):
                term = win[o, i] * p_in[op, o, i : i + 1, :]
                total = term if total is None else total + term
            terms.append(total)
        wu[op + 1] += folded(
            jnp.dot(
                stacked(jnp.concatenate(terms, axis=1)), nodes_recv[...],
                preferred_element_type=F32,
            )
        )

    def sums_send(op):
        values = folded(jnp.dot(stacked(wu[op]), nodes_t[...], preferred_element_type=F32))
        for o in range(n_ea):
            for i in range(comps):
                s_out[op, o, i : i + 1, :] = jnp.sum(
                    win[o, i] * values[:, slabs(o)], axis=0, keepdims=True
                )
        for d in range(1, n_ea):
            s_copy(op, d).start()

    def first_sums():
        w_in[ek] = wu[0]
        for d in range(1, n_ea):
            w_copy(d).wait_recv()
        for o in range(n_ea):
            values = folded(jnp.dot(stacked(w_in[o]), nodes_mine[o], preferred_element_type=F32))
            for i in range(comps):
                s_in[0, o, i : i + 1, :] = jnp.sum(
                    weights[o, i] * values, axis=0, keepdims=True
                )

    def sums_wait(op):
        s_in[op, ek] = s_out[op, ek]
        for d in range(1, n_ea):
            s_copy(op, d).wait_recv()

    def cells_step(op):
        spread_h, spread_l = [], []
        for i in range(comps):
            line = jnp.concatenate([s_in[op, o, i : i + 1, :] for o in range(n_ea)], axis=1)
            h, l = pieces(line)
            spread_h.append(rows_b[...] * h)
            spread_l.append(rows_b[...] * l)
        added = folded(
            jnp.dot(
                jnp.concatenate(spread_h + spread_l, axis=0), lanes_t[...],
                preferred_element_type=F32,
            )
        )
        z_low, z_high = z_in[op, 0], z_in[op, 1]
        for i in range(comps):
            for a in range(dx):
                at = i * dx + a
                low = jnp.where(row_i == 0, y_in[op, 0, at : at + 1, :], 0.0)
                high = jnp.where(row_i == dy - 1, y_in[op, 1, at : at + 1, :], 0.0)
                side = low + high
                z_l, z_h = [], []
                for b in range(dy // 8):
                    g = at * (dy // 8) + b
                    z_l.append(jnp.broadcast_to(z_low[:, g : g + 1], (8, dz)))
                    z_h.append(jnp.broadcast_to(z_high[:, g : g + 1], (8, dz)))
                side = side + jnp.where(lane_b == 0, jnp.concatenate(z_l, axis=0), 0.0)
                side = side + jnp.where(lane_b == dz - 1, jnp.concatenate(z_h, axis=0), 0.0)
                if a == 0:
                    side = side + x_in[op, 0, i]
                if a == dx - 1:
                    side = side + x_in[op, 1, i]
                vu[op + 1, i, a] += added[at * dy : (at + 1) * dy] - side

    def last_moment(op, row):
        x_low = x_in[op, 0] * vu[op, :, 0]
        x_high = x_in[op, 1] * vu[op, :, dx - 1]
        side = jnp.sum((x_low + x_high).reshape(comps * dy, dz), axis=0, keepdims=True)
        y = y_out[op, 1, :edge_rows] * y_in[op, 0, :edge_rows]
        y = y + y_out[op, 0, :edge_rows] * y_in[op, 1, :edge_rows]
        side = side + jnp.sum(y, axis=0, keepdims=True)
        z = z_out[op, 1] * z_in[op, 0] + z_out[op, 0] * z_in[op, 1]
        side = side + jnp.sum(z, axis=0, keepdims=True)
        cross = None
        for o in range(n_ea):
            term = p_out[op, o] * s_in[op, o]
            cross = term if cross is None else cross + term
        cross = jnp.sum(cross, axis=0, keepdims=True)
        return row - side + 2.0 * cross

    loads["cell"].wait()
    tile = cell[0]
    tile_row = lax.div(tile, dz)
    tile_lane = tile - tile_row * dz
    for o in range(n_ea):
        lanes[:, slabs(o)] = jnp.where(
            iota((dz, cap), 0) == tile_lane[o : o + 1], 1.0, 0.0
        ).astype(BF16)
        r = jnp.where(iota((per, cap), 0) == tile_row[o : o + 1], 1.0, 0.0)
        rows[:, slabs(o)] = r
        rows_b[:, slabs(o)] = r.astype(BF16)
    loads["v"].wait()
    halo_pack(0)
    pick(0)
    loads["w"].wait()
    wu[0] = jnp.concatenate([w_first[...], jnp.zeros((epad - ecomp, enb), F32)], axis=0)
    for name in ("node", "kind", "coupling"):
        loads[name].wait()

    pl.semaphore_wait(barrier, expected)

    for d in range(1, n_ea):
        w_copy(d).start()
    halo_send(0)
    pick_send(0)
    for d in range(1, n_ea):
        for copy in table_copies(d):
            copy.start()

    lane_columns = columns(tile_lane)
    for o in range(n_ea):
        lanes_t[slabs(o), :] = jnp.where(
            iota((cap, dz), 1) == lane_columns[:, o : o + 1], 1.0, 0.0
        ).astype(BF16)
        nodes_mine[o] = jnp.where(
            iota((enb, cap), 0) == node[0, o : o + 1, :], 1.0, 0.0
        ).astype(BF16)
    no_row = jnp.zeros((epad - ecomp, cap), F32)

    def masked(raw, k):
        heavi = jnp.where(k >= 1, 1.0, 0.0)
        tip = jnp.where(k == 2, 1.0, 0.0)
        mask = jnp.where(iota((ecomp, cap), 0) < 3, heavi, tip)
        return jnp.concatenate([raw * mask, no_row], axis=0)

    for o in range(n_ea):
        for i in range(comps):
            weights[o, i] = masked(coupling[i, :, slabs(o)], kind[0, o : o + 1, :])
    loads["off"].wait()
    loads["diag"].wait()
    for p in range(ecomp):
        whole = 0.5 * (off[p] + off[:, p, :])
        whole = jnp.where(iota((ecomp, enb), 0) == p, diag[p : p + 1, :] - CENTRE, whole)
        stiff[p] = jnp.concatenate([whole, jnp.zeros((epad - ecomp, enb), F32)], axis=0)
    loads["shift"].wait()
    centre_diag[...] = shift[...] + (6.0 - CENTRE)
    node_in[ek] = node[...]
    kind_in[ek] = kind[...]
    coup_in[ek] = coupling[:, :, block(0)]
    local(0)
    local_nodes(0)
    moments = [product(0, 0)]

    first_sums()
    halo_wait(0)
    cells_step(0)
    halo_pack(1)
    halo_send(1)
    pick(1)
    pick_send(1)

    for d in range(1, n_ea):
        for copy in table_copies(d):
            copy.wait_recv()
    own_rows = jnp.concatenate(
        [node_in[o, 0, pl.ds(ek, 1), :] for o in range(n_ea)], axis=0
    )
    node_columns = columns(own_rows)
    for o in range(n_ea):
        nodes_recv[slabs(o), :] = jnp.where(
            iota((cap, enb), 1) == node_columns[:, o : o + 1], 1.0, 0.0
        ).astype(BF16)
        nodes_t[:, slabs(o)] = jnp.where(
            iota((enb, cap), 0) == own_rows[o : o + 1, :], 1.0, 0.0
        ).astype(BF16)
        for i in range(comps):
            win[o, i] = masked(coup_in[o, i], kind_in[o, 0, pl.ds(ek, 1), :])
    nodes_step(0)
    sums_send(1)
    last = ITERS - 1
    for op in range(1, last):
        moments.append(product(op - 1, op))
        moments.append(product(op, op))
        local(op)
        local_nodes(op)
        nodes_step(op)
        sums_send(op + 1)
        halo_wait(op)
        sums_wait(op)
        cells_step(op)
        halo_pack(op + 1)
        halo_send(op + 1)
        pick(op + 1)
        pick_send(op + 1)

    moments.append(product(last - 1, last))
    moments.append(product(last, last))
    local(last)
    local_nodes(last)
    row = product(last, last + 1)
    packed = jnp.zeros((1, dz), F32)
    for n, m in enumerate(moments):
        packed = jnp.where(lane_r == n, jnp.sum(m, axis=1, keepdims=True), packed)
    halo_wait(last)
    sums_wait(last)
    row = last_moment(last, row)
    at = 2 * ITERS - 1
    packed = jnp.where(lane_r == at, jnp.sum(row, axis=1, keepdims=True), packed)

    def red_copy(stage, me, target, d):
        return remote(
            red_out.at[stage], red.at[stage, me], red_s.at[stage, d], red_r.at[stage, d],
            target(d),
        )

    for stage, group in enumerate(groups):
        total, me, target = members(group)
        red_out[stage] = packed
        for d in range(1, total):
            red_copy(stage, me, target, d).start()
        red[stage, me] = packed
        if stage == 0:
            cells_step(last)
            nodes_step(last)
            for op in range(ITERS):
                for s in (1, -1):
                    for name, copy in (("gx", x_copy), ("gy", y_copy), ("ea", z_copy)):
                        @pl.when(has[name, s])
                        def _():
                            copy(op, s).wait_send()
                for d in range(1, n_ea):
                    p_copy(op, d).wait_send()
                    if op > 0:
                        s_copy(op, d).wait_send()
            for d in range(1, n_ea):
                w_copy(d).wait_send()
                for copy in table_copies(d):
                    copy.wait_send()
        for d in range(1, total):
            red_copy(stage, me, target, d).wait_send()
        for d in range(1, total):
            red_copy(stage, me, target, d).wait_recv()
        packed = jnp.sum(red[stage, :total], axis=0)

    sol, res = cg_coefficients([packed[:, n : n + 1] for n in range(2 * ITERS)])
    tile = jnp.zeros((1, dz), F32)
    for n, c in enumerate(sol + res):
        tile = jnp.where(lane_r == n, c, tile)
    coefs[...] = tile


def combine_kernel(vu, wu, coefs, sol_v, res_v, sol_w, res_w):
    ecomp = sol_w.shape[0]
    tile = coefs[...]
    solution = [tile[:, n : n + 1] for n in range(ITERS)]
    residual = [tile[:, ITERS + n : ITERS + n + 1] for n in range(ITERS + 1)]

    def combine(factors, terms):
        out = factors[0] * terms[0]
        for f, t in zip(factors[1:], terms[1:]):
            out = out + f * t
        return out

    shape = sol_v.shape
    flat = (shape[0] * shape[1] * shape[2], shape[3])
    v_terms = [vu[n].reshape(flat) for n in range(ITERS + 1)]
    w_terms = [wu[n] for n in range(ITERS + 1)]
    sol_v[...] = combine(solution, v_terms).reshape(shape)
    res_v[...] = combine(residual, v_terms).reshape(shape)
    sol_w[...] = combine(solution, w_terms)[:ecomp]
    res_w[...] = combine(residual, w_terms)[:ecomp]


def body(sizes, *args):
    load_v, load_w, shift, diag, off, coupling, kind, cell, node = args
    n_ea = sizes[2]
    total = sizes[0] * sizes[1] * sizes[2]
    groups = (AXES,) if total <= 64 else (("gx",), ("gy", "ea"))
    widest = total if total <= 64 else max(sizes[0], sizes[1] * sizes[2])
    comps, dx, dy, dz = load_v.shape
    ecomp, enb = load_w.shape
    cap = node.shape[2]
    vmem = pltpu.VMEM
    dma = pltpu.SemaphoreType.DMA
    y_rows = -(-comps * dx // 8) * 8
    epad = -(-ecomp // 16) * 16
    slots = n_ea * cap
    scratch = [
        vmem(load_w.shape, F32), vmem(shift.shape, F32), vmem(diag.shape, F32),
        vmem(off.shape, F32), vmem(coupling.shape, F32),
        vmem(kind.shape, jnp.int32), vmem(cell.shape, jnp.int32), vmem(node.shape, jnp.int32),
        dma((9,)),
        vmem((n_ea, comps, epad, cap), F32),
        vmem((n_ea, comps, epad, cap), F32),
        vmem((ecomp, epad, enb), F32),
        vmem((dz, slots), BF16),
        vmem((slots, dz), BF16),
        vmem((dx * dy, slots), F32),
        vmem((dx * dy, slots), BF16),
        vmem((n_ea, enb, cap), BF16),
        vmem((slots, enb), BF16),
        vmem((enb, slots), BF16),
        vmem((dx, dy, dz), F32),
        vmem((n_ea,) + node.shape, jnp.int32),
        vmem((n_ea,) + kind.shape, jnp.int32),
        vmem((n_ea, comps, ecomp, cap), F32),
        vmem((ITERS, 2, comps, dy, dz), F32),
        vmem((ITERS, 2, y_rows, dz), F32),
        vmem((ITERS, 2, 8, dz), F32),
        vmem((n_ea, epad, enb), F32),
        vmem((ITERS, n_ea, comps, cap), F32),
        vmem((ITERS, n_ea, comps, cap), F32),
        vmem((ITERS, 2, y_rows, dz), F32),
        vmem((ITERS, 2, 8, dz), F32),
        vmem((ITERS, n_ea, comps, cap), F32),
        vmem((ITERS, n_ea, comps, cap), F32),
        vmem((len(groups), widest, 1, dz), F32),
        vmem((len(groups), 1, dz), F32),
        dma((n_ea,)), dma((n_ea,)),
        dma((n_ea,)), dma((n_ea,)),
        dma((n_ea,)), dma((n_ea,)),
        dma((ITERS, 2)), dma((ITERS, 2)),
        dma((ITERS, 2)), dma((ITERS, 2)),
        dma((ITERS, 2)), dma((ITERS, 2)),
        dma((n_ea,)), dma((n_ea,)),
        dma((ITERS, n_ea)), dma((ITERS, n_ea)),
        dma((ITERS, n_ea)), dma((ITERS, n_ea)),
        dma((len(groups), widest)), dma((len(groups), widest)),
    ]
    basis = pl.pallas_call(
        functools.partial(kernel, sizes, groups),
        out_shape=(
            pltpu.VMEM((ITERS + 1,) + load_v.shape, F32),
            pltpu.VMEM((ITERS + 1, epad, enb), F32),
            pltpu.VMEM((1, dz), F32),
        ),
        in_specs=[pl.BlockSpec(memory_space=pltpu.HBM)] * 9,
        out_specs=[pl.BlockSpec(memory_space=vmem)] * 3,
        scratch_shapes=scratch,
        compiler_params=pltpu.CompilerParams(
            collective_id=0, has_side_effects=True
        ),
        name="krylov",
    )(*args)
    return tuple(
        pl.pallas_call(
            combine_kernel,
            out_shape=tuple(
                jax.ShapeDtypeStruct(like.shape, F32)
                for like in (load_v, load_v, load_w, load_w)
            ),
            in_specs=[pl.BlockSpec(memory_space=vmem)] * 3,
            out_specs=[pl.BlockSpec(memory_space=vmem)] * 4,
            compiler_params=pltpu.CompilerParams(vmem_limit_bytes=8 << 20),
            name="combine",
        )(*basis)
    )


def solution(mesh):
    column = ("gx", "gy", "ea")
    placed = (
        P(None, "gx", "gy", "ea"),
        P(None, column),
        P("gx", "gy", "ea"),
        P(None, column),
        P(None, None, column),
        P(None, None, column),
        P(column, None, None),
        P(column, None, None),
        P(column, None, None),
    )
    return jax.shard_map(
        functools.partial(body, tuple(mesh.shape[a] for a in AXES)),
        mesh=mesh,
        in_specs=placed,
        out_specs=(
            P(None, "gx", "gy", "ea"),
            P(None, "gx", "gy", "ea"),
            P(None, column),
            P(None, column),
        ),
        check_vma=False,
    )
```

time: 24.6 us -> 23.6 us (0.959)
  Pallas kernels: 23.8 us -> 22.8 us
    pallas_call x1, Pallas kernels: 23 us -> 22 us  [body(): pl.pallas_call(functools.partial(kernel, sizes, groups), out_shape=(pltpu...]
where the time goes in v2:
time: 23.6 us; the launch traced here: 23.4 us
  Pallas kernels  22.8 us (97%)
  between operations  0.64 us (3%)
    pallas_call x1, Pallas kernels, body(): pl.pallas_call(functools.partial(kernel, sizes, groups), out_shape=(pltpu...  22 us
    pallas_call x1, Pallas kernels, body(): pl.pallas_call(combine_kernel, out_shape=tuple((jax.ShapeDtypeStruct(like...  0.78 us

profile of v2, /device:TPU:0, one launch (start us, length us, event | category | flops | bytes accessed | tf_op | source)
XLA Modules:
  0.0 23.4 jit_solution(966811587987112663)
XLA Ops:
  0.6 22.0 %krylov.1 = (f32[4,3,4,16,128]{4,3,2,1,0:T(8,128)S(1)}, f32[4,16,256]{2,1,0:T(8,128)S(1)}, f32[1,128]{1,0:T(1,128)S(1)}) custom-call(f32[3,4,16,128]{3,2,1,0:T(8,128)} %load_v.1, f32[15,256]{1,0:T(8,128)} %load_w.1, f32[4,16,128]{2,1,0:T(8,128)} %shift_h.1, f32[15,256]{1,0:T(8,128)} %diag_h.1, f32[15,15,256]{2,1,0:T(8,128)} %off_h.1, ...), custom_call_target="tpu_custom_call" | custom-call | tf_op jit(solution)/shard_map/krylov/pallas_call | solution.py:631
  22.6 0.8 %combine.1 = (f32[3,4,16,128]{3,2,1,0:T(8,128)}, f32[3,4,16,128]{3,2,1,0:T(8,128)}, f32[15,256]{1,0:T(8,128)}, f32[15,256]{1,0:T(8,128)}) custom-call(f32[4,3,4,16,128]{4,3,2,1,0:T(8,128)S(1)} %get-tuple-element.7.vu, f32[4,16,256]{2,1,0:T(8,128)S(1)} %get-tuple-element.8.wu, f32[1,128]{1,0:T(1,128)S(1)} %get-tuple-element.9.coefs), custom_call_target="tpu_custom_call" | custom-call | tf_op jit(solution)/shard_map/combine/pallas_call | solution.py:647

commit v3 on v2

--- a/solution.py
+++ b/solution.py
@@ -73,22 +73,21 @@
     sizes, groups,
     load_v, load_w, shift_h, diag_h, off_h, coupling_h, kind_h, cell_h, node_h,
     vu, wu, coefs,
-    w_first, shift, diag, off, coupling, kind, cell, node, load_s,
+    w_first, shift, diag, off, coupling, cell, ids, load_s,
     weights, win, stiff, lanes, lanes_t, rows, rows_b, nodes_mine, nodes_recv, nodes_t,
-    centre_diag, node_in, kind_in, coup_in,
-    x_in, y_in, z_in, w_in, p_in, s_in, y_out, z_out, p_out, s_out, red, red_out,
-    node_s, node_r, kind_s, kind_r, coup_s, coup_r,
+    centre_diag, ids_in, coup_in,
+    x_in, y_in, z_in, w_in, p_in, s_in, z_out, p_out, s_out, red, red_out,
+    ids_s, ids_r, coup_s, coup_r,
     x_s, x_r, y_s, y_r, z_s, z_r, w_s, w_r, p_s, p_r, s_s, s_r, red_s, red_r,
 ):
     n_gx, n_gy, n_ea = sizes
     comps, dx, dy, dz = load_v.shape
     ecomp, enb = load_w.shape
     epad = wu.shape[1]
-    cap = node.shape[2]
+    cap = cell.shape[2]
     per = dx * dy
     allrows = comps * per
     groups8 = allrows // 8
-    edge_rows = comps * dx
     gi, gj, ek = (lax.axis_index(a) for a in AXES)
     own = {"gx": gi, "gy": gj, "ea": ek}
     count = dict(zip(AXES, sizes))
@@ -142,10 +141,11 @@
 
     loads = {}
     for at, (name, src, dst) in enumerate((
-        ("cell", cell_h, cell), ("v", load_v, vu.at[0]), ("w", load_w, w_first),
-        ("node", node_h, node), ("kind", kind_h, kind), ("coupling", coupling_h, coupling),
+        ("w", load_w, w_first), ("node", node_h, ids.at[0]), ("kind", kind_h, ids.at[1]),
+        ("v", load_v, vu.at[0]), ("cell", cell_h, cell), ("coupling", coupling_h, coupling),
         ("shift", shift_h, shift), ("off", off_h, off), ("diag", diag_h, diag),
     )):
+        at = 1 if name == "kind" else at
         loads[name] = pltpu.make_async_copy(src, dst, load_s.at[at])
         loads[name].start()
 
@@ -165,49 +165,64 @@
             device_id=device, device_id_type=MESH,
         )
 
+    sides = {
+        name: jnp.where(has[name, 1], 1, 0) + jnp.where(has[name, -1], 1, 0) for name in AXES
+    }
+
+    def landed(ref, sem):
+        pltpu.make_async_copy(ref, ref, sem).wait()
+
     def x_copy(op, s):
         return remote(
             vu.at[op, :, dx - 1 if s == 1 else 0], x_in.at[op, slot[s]],
-            x_s.at[op, slot[s]], x_r.at[op, slot[s]], beside["gx", s],
+            x_s.at[0], x_r.at[op], beside["gx", s],
         )
 
     def y_copy(op, s):
+        edge = dy - 1 if s == 1 else 0
         return remote(
-            y_out.at[op, slot[s]], y_in.at[op, slot[s]],
-            y_s.at[op, slot[s]], y_r.at[op, slot[s]], beside["gy", s],
+            vu.at[op, :, :, edge : edge + 1, :], y_in.at[op, slot[s]],
+            y_s.at[0], y_r.at[op], beside["gy", s],
         )
 
     def z_copy(op, s):
         return remote(
             z_out.at[op, slot[s]], z_in.at[op, slot[s]],
-            z_s.at[op, slot[s]], z_r.at[op, slot[s]], beside["ea", s],
+            z_s.at[0], z_r.at[op], beside["ea", s],
         )
 
     def column_copy(src, dst, s_sem, r_sem, d):
-        return remote(src, dst.at[ek], s_sem.at[d], r_sem.at[d], (gi, gj, partner(d)))
+        return remote(src, dst.at[ek], s_sem, r_sem, (gi, gj, partner(d)))
 
     def w_copy(d):
-        return column_copy(wu.at[0], w_in, w_s, w_r, d)
+        return column_copy(wu.at[0], w_in, w_s.at[0], w_r.at[0], d)
 
     def p_copy(op, d):
         return column_copy(
-            p_out.at[op, partner(d)], p_in.at[op], p_s.at[op], p_r.at[op], d
+            p_out.at[op, partner(d)], p_in.at[op], p_s.at[0], p_r.at[op], d
         )
 
     def s_copy(op, d):
         return column_copy(
-            s_out.at[op, partner(d)], s_in.at[op], s_s.at[op], s_r.at[op], d
+            s_out.at[op, partner(d)], s_in.at[op], s_s.at[0], s_r.at[op], d
+        )
+
+    def ids_copy(d):
+        return column_copy(
+            ids.at[:, 0, pl.ds(partner(d), 1), :], ids_in, ids_s.at[0], ids_r.at[0], d
         )
 
     def block(d):
         return pl.ds(pl.multiple_of(partner(d) * cap, cap), cap)
 
-    def table_copies(d):
-        return (
-            column_copy(node, node_in, node_s, node_r, d),
-            column_copy(kind, kind_in, kind_s, kind_r, d),
-            column_copy(coupling.at[:, :, block(d)], coup_in, coup_s, coup_r, d),
-        )
+    def coup_copy(d):
+        return column_copy(
+            coupling.at[:, :, block(d)], coup_in, coup_s.at[0], coup_r.at[0], d
+        )
+
+    def column_send(copy):
+        for d in range(1, n_ea):
+            copy(d).start()
 
     lane_i = iota((8, dz), 1)
     lane_r = iota((1, dz), 1)
@@ -223,13 +238,13 @@
     def slabs(o):
         return slice(o * cap, (o + 1) * cap)
 
-    def halo_pack(op):
+    def halo_send(op):
+        for s in (1, -1):
+            for name, copy in (("gx", x_copy), ("gy", y_copy)):
+                @pl.when(has[name, s])
+                def _():
+                    copy(op, s).start()
         v2 = vu[op].reshape(allrows, dz)
-        for i in range(comps):
-            for a in range(dx):
-                at = i * dx + a
-                y_out[op, 0, at : at + 1, :] = vu[op, i, a, dy - 1 : dy, :]
-                y_out[op, 1, at : at + 1, :] = vu[op, i, a, 0:1, :]
         up = jnp.zeros((8, dz), F32)
         down = jnp.zeros((8, dz), F32)
         for g in range(groups8):
@@ -238,32 +253,42 @@
             down = jnp.where(lane_i == g, part[:, 0:1], down)
         z_out[op, 0] = up
         z_out[op, 1] = down
-
-    def halo_send(op):
         for s in (1, -1):
-            for name, copy in (("gx", x_copy), ("gy", y_copy), ("ea", z_copy)):
-                @pl.when(has[name, s])
-                def _():
-                    copy(op, s).start()
+            @pl.when(has["ea", s])
+            def _():
+                z_copy(op, s).start()
+
+    def by_sides(name, two, one, sem):
+        @pl.when(sides[name] == 2)
+        def _():
+            landed(two, sem)
+
+        @pl.when(sides[name] == 1)
+        def _():
+            landed(one, sem)
 
     def halo_wait(op):
-        for s in (1, -1):
-            for name, copy in (("gx", x_copy), ("gy", y_copy), ("ea", z_copy)):
-                @pl.when(has[name, -s])
-                def _():
-                    copy(op, s).wait_recv()
+        for name, buffer, sem in (("gx", x_in, x_r), ("gy", y_in, y_r), ("ea", z_in, z_r)):
+            by_sides(name, buffer.at[op], buffer.at[op, 0], sem.at[op])
 
     def pick(op):
-        v2 = vu[op].reshape(allrows, dz)
-        seen = folded(jnp.dot(stacked(v2), lanes[...], preferred_element_type=F32))
+        h, l = pieces(vu[op].reshape(allrows, dz))
+        seen = jnp.dot(
+            jnp.concatenate([h, l], axis=1), lanes[...], preferred_element_type=F32
+        )
+        return [
+            jnp.sum(seen[i * per : (i + 1) * per] * rows[...], axis=0, keepdims=True)
+            for i in range(comps)
+        ]
+
+    def pick_send(op, picked):
         for i in range(comps):
-            picked = jnp.sum(seen[i * per : (i + 1) * per] * rows[...], axis=0, keepdims=True)
             for o in range(n_ea):
-                p_out[op, o, i : i + 1, :] = picked[:, slabs(o)]
-
-    def pick_send(op):
-        for d in range(1, n_ea):
-            p_copy(op, d).start()
+                line = picked[i][:, slabs(o)]
+                if op > 0:
+                    line = line + s_in[op - 1, o, i : i + 1, :]
+                p_out[op, o, i : i + 1, :] = line
+        column_send(functools.partial(p_copy, op))
 
     def local(op):
         v4 = vu[op]
@@ -298,8 +323,7 @@
 
     def nodes_step(op):
         p_in[op, ek] = p_out[op, ek]
-        for d in range(1, n_ea):
-            p_copy(op, d).wait_recv()
+        landed(p_in.at[op, : n_ea - 1], p_r.at[op])
         terms = []
         for o in range(n_ea):
             total = None
@@ -321,13 +345,11 @@
                 s_out[op, o, i : i + 1, :] = jnp.sum(
                     win[o, i] * values[:, slabs(o)], axis=0, keepdims=True
                 )
-        for d in range(1, n_ea):
-            s_copy(op, d).start()
+        column_send(functools.partial(s_copy, op))
 
     def first_sums():
         w_in[ek] = wu[0]
-        for d in range(1, n_ea):
-            w_copy(d).wait_recv()
+        landed(w_in.at[: n_ea - 1], w_r.at[0])
         for o in range(n_ea):
             values = folded(jnp.dot(stacked(w_in[o]), nodes_mine[o], preferred_element_type=F32))
             for i in range(comps):
@@ -337,8 +359,27 @@
 
     def sums_wait(op):
         s_in[op, ek] = s_out[op, ek]
-        for d in range(1, n_ea):
-            s_copy(op, d).wait_recv()
+        landed(s_in.at[op, : n_ea - 1], s_r.at[op])
+
+    def halo_apply(op):
+        z_low, z_high = z_in[op, 0], z_in[op, 1]
+        for i in range(comps):
+            for a in range(dx):
+                at = i * dx + a
+                side = jnp.where(row_i == 0, y_in[op, 0, i, a], 0.0)
+                side = side + jnp.where(row_i == dy - 1, y_in[op, 1, i, a], 0.0)
+                z_l, z_h = [], []
+                for b in range(dy // 8):
+                    g = at * (dy // 8) + b
+                    z_l.append(jnp.broadcast_to(z_low[:, g : g + 1], (8, dz)))
+                    z_h.append(jnp.broadcast_to(z_high[:, g : g + 1], (8, dz)))
+                side = side + jnp.where(lane_b == 0, jnp.concatenate(z_l, axis=0), 0.0)
+                side = side + jnp.where(lane_b == dz - 1, jnp.concatenate(z_h, axis=0), 0.0)
+                if a == 0:
+                    side = side + x_in[op, 0, i]
+                if a == dx - 1:
+                    side = side + x_in[op, 1, i]
+                vu[op + 1, i, a] -= side
 
     def cells_step(op):
         spread_h, spread_l = [], []
@@ -353,33 +394,14 @@
                 preferred_element_type=F32,
             )
         )
-        z_low, z_high = z_in[op, 0], z_in[op, 1]
-        for i in range(comps):
-            for a in range(dx):
-                at = i * dx + a
-                low = jnp.where(row_i == 0, y_in[op, 0, at : at + 1, :], 0.0)
-                high = jnp.where(row_i == dy - 1, y_in[op, 1, at : at + 1, :], 0.0)
-                side = low + high
-                z_l, z_h = [], []
-                for b in range(dy // 8):
-                    g = at * (dy // 8) + b
-                    z_l.append(jnp.broadcast_to(z_low[:, g : g + 1], (8, dz)))
-                    z_h.append(jnp.broadcast_to(z_high[:, g : g + 1], (8, dz)))
-                side = side + jnp.where(lane_b == 0, jnp.concatenate(z_l, axis=0), 0.0)
-                side = side + jnp.where(lane_b == dz - 1, jnp.concatenate(z_h, axis=0), 0.0)
-                if a == 0:
-                    side = side + x_in[op, 0, i]
-                if a == dx - 1:
-                    side = side + x_in[op, 1, i]
-                vu[op + 1, i, a] += added[at * dy : (at + 1) * dy] - side
+        vu[op + 1] += added.reshape(comps, dx, dy, dz)
 
     def last_moment(op, row):
         x_low = x_in[op, 0] * vu[op, :, 0]
         x_high = x_in[op, 1] * vu[op, :, dx - 1]
         side = jnp.sum((x_low + x_high).reshape(comps * dy, dz), axis=0, keepdims=True)
-        y = y_out[op, 1, :edge_rows] * y_in[op, 0, :edge_rows]
-        y = y + y_out[op, 0, :edge_rows] * y_in[op, 1, :edge_rows]
-        side = side + jnp.sum(y, axis=0, keepdims=True)
+        y = y_in[op, 0] * vu[op, :, :, 0:1] + y_in[op, 1] * vu[op, :, :, dy - 1 : dy]
+        side = side + jnp.sum(y.reshape(comps * dx, dz), axis=0, keepdims=True)
         z = z_out[op, 1] * z_in[op, 0] + z_out[op, 0] * z_in[op, 1]
         side = side + jnp.sum(z, axis=0, keepdims=True)
         cross = None
@@ -389,34 +411,32 @@
         cross = jnp.sum(cross, axis=0, keepdims=True)
         return row - side + 2.0 * cross
 
+    loads["w"].wait()
+    wu[0] = jnp.concatenate([w_first[...], jnp.zeros((epad - ecomp, enb), F32)], axis=0)
+    landed(ids, load_s.at[1])
+    loads["v"].wait()
+
+    pl.semaphore_wait(barrier, expected)
+
+    column_send(ids_copy)
+    column_send(w_copy)
+    halo_send(0)
     loads["cell"].wait()
     tile = cell[0]
     tile_row = lax.div(tile, dz)
     tile_lane = tile - tile_row * dz
     for o in range(n_ea):
-        lanes[:, slabs(o)] = jnp.where(
+        hot = jnp.where(
             iota((dz, cap), 0) == tile_lane[o : o + 1], 1.0, 0.0
         ).astype(BF16)
+        lanes[:dz, slabs(o)] = hot
+        lanes[dz:, slabs(o)] = hot
         r = jnp.where(iota((per, cap), 0) == tile_row[o : o + 1], 1.0, 0.0)
         rows[:, slabs(o)] = r
         rows_b[:, slabs(o)] = r.astype(BF16)
-    loads["v"].wait()
-    halo_pack(0)
-    pick(0)
-    loads["w"].wait()
-    wu[0] = jnp.concatenate([w_first[...], jnp.zeros((epad - ecomp, enb), F32)], axis=0)
-    for name in ("node", "kind", "coupling"):
-        loads[name].wait()
-
-    pl.semaphore_wait(barrier, expected)
-
-    for d in range(1, n_ea):
-        w_copy(d).start()
-    halo_send(0)
-    pick_send(0)
-    for d in range(1, n_ea):
-        for copy in table_copies(d):
-            copy.start()
+    pick_send(0, pick(0))
+    loads["coupling"].wait()
+    column_send(coup_copy)
 
     lane_columns = columns(tile_lane)
     for o in range(n_ea):
@@ -424,7 +444,7 @@
             iota((cap, dz), 1) == lane_columns[:, o : o + 1], 1.0, 0.0
         ).astype(BF16)
         nodes_mine[o] = jnp.where(
-            iota((enb, cap), 0) == node[0, o : o + 1, :], 1.0, 0.0
+            iota((enb, cap), 0) == ids[0, 0, o : o + 1, :], 1.0, 0.0
         ).astype(BF16)
     no_row = jnp.zeros((epad - ecomp, cap), F32)
 
@@ -436,36 +456,22 @@
 
     for o in range(n_ea):
         for i in range(comps):
-            weights[o, i] = masked(coupling[i, :, slabs(o)], kind[0, o : o + 1, :])
+            weights[o, i] = masked(coupling[i, :, slabs(o)], ids[1, 0, o : o + 1, :])
+    loads["shift"].wait()
+    centre_diag[...] = shift[...] + (6.0 - CENTRE)
+    local(0)
     loads["off"].wait()
     loads["diag"].wait()
     for p in range(ecomp):
         whole = 0.5 * (off[p] + off[:, p, :])
         whole = jnp.where(iota((ecomp, enb), 0) == p, diag[p : p + 1, :] - CENTRE, whole)
         stiff[p] = jnp.concatenate([whole, jnp.zeros((epad - ecomp, enb), F32)], axis=0)
-    loads["shift"].wait()
-    centre_diag[...] = shift[...] + (6.0 - CENTRE)
-    node_in[ek] = node[...]
-    kind_in[ek] = kind[...]
-    coup_in[ek] = coupling[:, :, block(0)]
-    local(0)
     local_nodes(0)
     moments = [product(0, 0)]
-
-    first_sums()
-    halo_wait(0)
-    cells_step(0)
-    halo_pack(1)
-    halo_send(1)
-    pick(1)
-    pick_send(1)
-
-    for d in range(1, n_ea):
-        for copy in table_copies(d):
-            copy.wait_recv()
-    own_rows = jnp.concatenate(
-        [node_in[o, 0, pl.ds(ek, 1), :] for o in range(n_ea)], axis=0
-    )
+    ids_in[ek] = ids[:, 0, pl.ds(ek, 1), :]
+    coup_in[ek] = coupling[:, :, block(0)]
+    landed(ids_in.at[: n_ea - 1], ids_r.at[0])
+    own_rows = jnp.concatenate([ids_in[o, 0] for o in range(n_ea)], axis=0)
     node_columns = columns(own_rows)
     for o in range(n_ea):
         nodes_recv[slabs(o), :] = jnp.where(
@@ -474,30 +480,40 @@
         nodes_t[:, slabs(o)] = jnp.where(
             iota((enb, cap), 0) == own_rows[o : o + 1, :], 1.0, 0.0
         ).astype(BF16)
+
+    halo_wait(0)
+    halo_apply(0)
+    picked = pick(1)
+    first_sums()
+    pick_send(1, picked)
+    cells_step(0)
+    halo_send(1)
+    landed(coup_in.at[: n_ea - 1], coup_r.at[0])
+    for o in range(n_ea):
         for i in range(comps):
-            win[o, i] = masked(coup_in[o, i], kind_in[o, 0, pl.ds(ek, 1), :])
+            win[o, i] = masked(coup_in[o, i], ids_in[o, 1])
     nodes_step(0)
     sums_send(1)
     last = ITERS - 1
     for op in range(1, last):
+        local(op)
+        local_nodes(op)
         moments.append(product(op - 1, op))
         moments.append(product(op, op))
-        local(op)
-        local_nodes(op)
+        halo_wait(op)
+        halo_apply(op)
+        picked = pick(op + 1)
+        sums_wait(op)
+        pick_send(op + 1, picked)
+        cells_step(op)
+        halo_send(op + 1)
         nodes_step(op)
         sums_send(op + 1)
-        halo_wait(op)
-        sums_wait(op)
-        cells_step(op)
-        halo_pack(op + 1)
-        halo_send(op + 1)
-        pick(op + 1)
-        pick_send(op + 1)
-
+
+    local(last)
+    local_nodes(last)
     moments.append(product(last - 1, last))
     moments.append(product(last, last))
-    local(last)
-    local_nodes(last)
     row = product(last, last + 1)
     packed = jnp.zeros((1, dz), F32)
     for n, m in enumerate(moments):
@@ -508,39 +524,35 @@
     at = 2 * ITERS - 1
     packed = jnp.where(lane_r == at, jnp.sum(row, axis=1, keepdims=True), packed)
 
-    def red_copy(stage, me, target, d):
-        return remote(
-            red_out.at[stage], red.at[stage, me], red_s.at[stage, d], red_r.at[stage, d],
-            target(d),
-        )
-
     for stage, group in enumerate(groups):
         total, me, target = members(group)
+        whole = group == AXES
         red_out[stage] = packed
-        for d in range(1, total):
-            red_copy(stage, me, target, d).start()
+        for d in range(total - 1):
+            dst = red.at[stage, me]
+            ends = (red_s.at[stage], red_r.at[stage])
+            if whole:
+                pltpu.make_async_remote_copy(
+                    src_ref=red_out.at[stage], dst_ref=dst, send_sem=ends[0], recv_sem=ends[1],
+                    device_id=d + jnp.where(me <= d, 1, 0),
+                    device_id_type=pl.DeviceIdType.LOGICAL,
+                ).start()
+            else:
+                remote(red_out.at[stage], dst, *ends, target(d + 1)).start()
         red[stage, me] = packed
         if stage == 0:
+            halo_apply(last)
             cells_step(last)
             nodes_step(last)
-            for op in range(ITERS):
-                for s in (1, -1):
-                    for name, copy in (("gx", x_copy), ("gy", y_copy), ("ea", z_copy)):
-                        @pl.when(has[name, s])
-                        def _():
-                            copy(op, s).wait_send()
-                for d in range(1, n_ea):
-                    p_copy(op, d).wait_send()
-                    if op > 0:
-                        s_copy(op, d).wait_send()
-            for d in range(1, n_ea):
-                w_copy(d).wait_send()
-                for copy in table_copies(d):
-                    copy.wait_send()
-        for d in range(1, total):
-            red_copy(stage, me, target, d).wait_send()
-        for d in range(1, total):
-            red_copy(stage, me, target, d).wait_recv()
+            for name, buffer, sem in (("gx", x_in, x_s), ("gy", y_in, y_s), ("ea", z_in, z_s)):
+                by_sides(name, buffer, buffer.at[:, 0], sem.at[0])
+            landed(p_in.at[:, : n_ea - 1], p_s.at[0])
+            landed(s_in.at[1:, : n_ea - 1], s_s.at[0])
+            landed(w_in.at[: n_ea - 1], w_s.at[0])
+            landed(ids_in.at[: n_ea - 1], ids_s.at[0])
+            landed(coup_in.at[: n_ea - 1], coup_s.at[0])
+        landed(red.at[stage, : total - 1], red_s.at[stage])
+        landed(red.at[stage, : total - 1], red_r.at[stage])
         packed = jnp.sum(red[stage, :total], axis=0)
 
     sol, res = cg_coefficients([packed[:, n : n + 1] for n in range(2 * ITERS)])
@@ -583,18 +595,17 @@
     cap = node.shape[2]
     vmem = pltpu.VMEM
     dma = pltpu.SemaphoreType.DMA
-    y_rows = -(-comps * dx // 8) * 8
     epad = -(-ecomp // 16) * 16
     slots = n_ea * cap
     scratch = [
         vmem(load_w.shape, F32), vmem(shift.shape, F32), vmem(diag.shape, F32),
         vmem(off.shape, F32), vmem(coupling.shape, F32),
-        vmem(kind.shape, jnp.int32), vmem(cell.shape, jnp.int32), vmem(node.shape, jnp.int32),
+        vmem(cell.shape, jnp.int32), vmem((2,) + node.shape, jnp.int32),
         dma((9,)),
         vmem((n_ea, comps, epad, cap), F32),
         vmem((n_ea, comps, epad, cap), F32),
         vmem((ecomp, epad, enb), F32),
-        vmem((dz, slots), BF16),
+        vmem((2 * dz, slots), BF16),
         vmem((slots, dz), BF16),
         vmem((dx * dy, slots), F32),
         vmem((dx * dy, slots), BF16),
@@ -602,31 +613,28 @@
         vmem((slots, enb), BF16),
         vmem((enb, slots), BF16),
         vmem((dx, dy, dz), F32),
-        vmem((n_ea,) + node.shape, jnp.int32),
-        vmem((n_ea,) + kind.shape, jnp.int32),
+        vmem((n_ea, 2, 1, cap), jnp.int32),
         vmem((n_ea, comps, ecomp, cap), F32),
         vmem((ITERS, 2, comps, dy, dz), F32),
-        vmem((ITERS, 2, y_rows, dz), F32),
+        vmem((ITERS, 2, comps, dx, 1, dz), F32),
         vmem((ITERS, 2, 8, dz), F32),
         vmem((n_ea, epad, enb), F32),
         vmem((ITERS, n_ea, comps, cap), F32),
         vmem((ITERS, n_ea, comps, cap), F32),
-        vmem((ITERS, 2, y_rows, dz), F32),
         vmem((ITERS, 2, 8, dz), F32),
         vmem((ITERS, n_ea, comps, cap), F32),
         vmem((ITERS, n_ea, comps, cap), F32),
         vmem((len(groups), widest, 1, dz), F32),
         vmem((len(groups), 1, dz), F32),
-        dma((n_ea,)), dma((n_ea,)),
-        dma((n_ea,)), dma((n_ea,)),
-        dma((n_ea,)), dma((n_ea,)),
-        dma((ITERS, 2)), dma((ITERS, 2)),
-        dma((ITERS, 2)), dma((ITERS, 2)),
-        dma((ITERS, 2)), dma((ITERS, 2)),
-        dma((n_ea,)), dma((n_ea,)),
-        dma((ITERS, n_ea)), dma((ITERS, n_ea)),
-        dma((ITERS, n_ea)), dma((ITERS, n_ea)),
-        dma((len(groups), widest)), dma((len(groups), widest)),
+        dma((1,)), dma((1,)),
+        dma((1,)), dma((1,)),
+        dma((1,)), dma((ITERS,)),
+        dma((1,)), dma((ITERS,)),
+        dma((1,)), dma((ITERS,)),
+        dma((1,)), dma((1,)),
+        dma((1,)), dma((ITERS,)),
+        dma((1,)), dma((ITERS,)),
+        dma((len(groups),)), dma((len(groups),)),
     ]
     basis = pl.pallas_call(
         functools.partial(kernel, sizes, groups),

time: 23.6 us -> 22 us (0.932)
  Pallas kernels: 22.8 us -> 21.1 us
    pallas_call x1, Pallas kernels: 22 us -> 20.4 us  [body(): pl.pallas_call(functools.partial(kernel, sizes, groups), out_shape=(pltpu...]
where the time goes in v3:
time: 22 us; the launch traced here: 21.8 us
  Pallas kernels  21.1 us (96%)
  between operations  0.64 us (3%)
    pallas_call x1, Pallas kernels, body(): pl.pallas_call(functools.partial(kernel, sizes, groups), out_shape=(pltpu...  20.4 us
    pallas_call x1, Pallas kernels, body(): pl.pallas_call(combine_kernel, out_shape=tuple((jax.ShapeDtypeStruct(like...  0.78 us

profile of v3, /device:TPU:0, one launch (start us, length us, event | category | flops | bytes accessed | tf_op | source)
XLA Modules:
  0.0 21.8 jit_solution(16507963472245989467)
XLA Ops:
  0.6 20.4 %krylov.1 = (f32[4,3,4,16,128]{4,3,2,1,0:T(8,128)S(1)}, f32[4,16,256]{2,1,0:T(8,128)S(1)}, f32[1,128]{1,0:T(1,128)S(1)}) custom-call(f32[3,4,16,128]{3,2,1,0:T(8,128)} %load_v.1, f32[15,256]{1,0:T(8,128)} %load_w.1, f32[4,16,128]{2,1,0:T(8,128)} %shift_h.1, f32[15,256]{1,0:T(8,128)} %diag_h.1, f32[15,15,256]{2,1,0:T(8,128)} %off_h.1, ...), custom_call_target="tpu_custom_call" | custom-call | tf_op jit(solution)/shard_map/krylov/pallas_call | solution.py:639
  21.0 0.8 %combine.1 = (f32[3,4,16,128]{3,2,1,0:T(8,128)}, f32[3,4,16,128]{3,2,1,0:T(8,128)}, f32[15,256]{1,0:T(8,128)}, f32[15,256]{1,0:T(8,128)}) custom-call(f32[4,3,4,16,128]{4,3,2,1,0:T(8,128)S(1)} %get-tuple-element.7.vu, f32[4,16,256]{2,1,0:T(8,128)S(1)} %get-tuple-element.8.wu, f32[1,128]{1,0:T(1,128)S(1)} %get-tuple-element.9.coefs), custom_call_target="tpu_custom_call" | custom-call | tf_op jit(solution)/shard_map/combine/pallas_call | solution.py:655

commit v4 on v3

--- a/solution.py
+++ b/solution.py
@@ -34,38 +34,29 @@
     return lax.broadcasted_iota(jnp.int32, shape, dim)
 
 
-def cg_coefficients(moment):
-    def inner(first, second):
-        total = None
-        for i, a in enumerate(first):
-            for j, b in enumerate(second):
-                term = a * b * moment[i + j]
-                total = term if total is None else total + term
-        return total
-
-    one = jnp.ones_like(moment[0])
-    residual, direction, solution = [one], [one], []
-    norm = moment[0]
-    for step in range(ITERS):
-        image = [CENTRE * d for d in direction] + [0.0 * one]
-        for i, d in enumerate(direction):
-            image[i + 1] = image[i + 1] + d
-        alpha = norm / inner(direction, image)
-        solution = [
-            (solution[i] if i < len(solution) else 0.0) + alpha * d
-            for i, d in enumerate(direction)
-        ]
-        residual = [
-            (residual[i] if i < len(residual) else 0.0) - alpha * d for i, d in enumerate(image)
-        ]
-        if step + 1 < ITERS:
-            new = inner(residual, residual)
-            ratio = new / norm
-            norm = new
-            direction = [
-                r + (ratio * direction[i] if i < len(direction) else 0.0)
-                for i, r in enumerate(residual)
-            ]
+def times_transposed(a, b):
+    return lax.dot_general(
+        a, b, (((1,), (1,)), ((), ())), preferred_element_type=F32
+    )
+
+
+def galerkin_coefficients(moment):
+    h = [moment[k + 1] + CENTRE * moment[k] for k in range(2 * ITERS - 1)]
+    first = 1.0 / h[0]
+    l1, l2 = h[1] * first, h[2] * first
+    d1 = h[2] - l1 * h[1]
+    e = h[3] - l1 * h[2]
+    g1 = moment[1] - l1 * moment[0]
+    second = 1.0 / d1
+    k = e * second
+    d2 = h[4] - l2 * h[2] - k * e
+    y2 = (moment[2] - l2 * moment[0] - k * g1) / d2
+    y1 = (g1 - e * y2) * second
+    y0 = (moment[0] - h[1] * y1 - h[2] * y2) * first
+    solution = [y0, y1, y2]
+    residual = [
+        1.0 - CENTRE * y0, -(y0 + CENTRE * y1), -(y1 + CENTRE * y2), -y2
+    ]
     return solution, residual
 
 
@@ -74,7 +65,7 @@
     load_v, load_w, shift_h, diag_h, off_h, coupling_h, kind_h, cell_h, node_h,
     vu, wu, coefs,
     w_first, shift, diag, off, coupling, cell, ids, load_s,
-    weights, win, stiff, lanes, lanes_t, rows, rows_b, nodes_mine, nodes_recv, nodes_t,
+    weights, win, stiff, lanes, rows, rows_b, nodes_mine, nodes_t,
     centre_diag, ids_in, coup_in,
     x_in, y_in, z_in, w_in, p_in, s_in, z_out, p_out, s_out, red, red_out,
     ids_s, ids_r, coup_s, coup_r,
@@ -229,21 +220,17 @@
     row_i = iota((dy, dz), 0)
     lane_b = iota((dy, dz), 1)
 
-    def columns(tile):
-        full = jnp.concatenate(
-            [tile.astype(F32), jnp.zeros((cap - tile.shape[0], cap), F32)], axis=0
-        )
-        return jnp.transpose(full).astype(jnp.int32)
-
     def slabs(o):
         return slice(o * cap, (o + 1) * cap)
 
-    def halo_send(op):
+    def xy_send(op):
         for s in (1, -1):
             for name, copy in (("gx", x_copy), ("gy", y_copy)):
                 @pl.when(has[name, s])
                 def _():
                     copy(op, s).start()
+
+    def z_send(op):
         v2 = vu[op].reshape(allrows, dz)
         up = jnp.zeros((8, dz), F32)
         down = jnp.zeros((8, dz), F32)
@@ -267,9 +254,12 @@
         def _():
             landed(one, sem)
 
-    def halo_wait(op):
-        for name, buffer, sem in (("gx", x_in, x_r), ("gy", y_in, y_r), ("ea", z_in, z_r)):
-            by_sides(name, buffer.at[op], buffer.at[op, 0], sem.at[op])
+    def x_wait(op):
+        by_sides("gx", x_in.at[op], x_in.at[op, 0], x_r.at[op])
+
+    def yz_wait(op):
+        by_sides("gy", y_in.at[op], y_in.at[op, 0], y_r.at[op])
+        by_sides("ea", z_in.at[op], z_in.at[op, 0], z_r.at[op])
 
     def pick(op):
         h, l = pieces(vu[op].reshape(allrows, dz))
@@ -281,13 +271,11 @@
             for i in range(comps)
         ]
 
-    def pick_send(op, picked):
+    def pick_send(op):
+        picked = pick(op)
         for i in range(comps):
             for o in range(n_ea):
-                line = picked[i][:, slabs(o)]
-                if op > 0:
-                    line = line + s_in[op - 1, o, i : i + 1, :]
-                p_out[op, o, i : i + 1, :] = line
+                p_out[op, o, i : i + 1, :] = picked[i][:, slabs(o)]
         column_send(functools.partial(p_copy, op))
 
     def local(op):
@@ -321,9 +309,11 @@
             total = total + pw[:, b * dz : (b + 1) * dz]
         return total
 
-    def nodes_step(op):
+    def picks_wait(op):
         p_in[op, ek] = p_out[op, ek]
         landed(p_in.at[op, : n_ea - 1], p_r.at[op])
+
+    def nodes_step(op):
         terms = []
         for o in range(n_ea):
             total = None
@@ -332,10 +322,7 @@
                 total = term if total is None else total + term
             terms.append(total)
         wu[op + 1] += folded(
-            jnp.dot(
-                stacked(jnp.concatenate(terms, axis=1)), nodes_recv[...],
-                preferred_element_type=F32,
-            )
+            times_transposed(stacked(jnp.concatenate(terms, axis=1)), nodes_t[...])
         )
 
     def sums_send(op):
@@ -361,7 +348,19 @@
         s_in[op, ek] = s_out[op, ek]
         landed(s_in.at[op, : n_ea - 1], s_r.at[op])
 
-    def halo_apply(op):
+    def cells_step(op):
+        spread_h, spread_l = [], []
+        for i in range(comps):
+            line = jnp.concatenate([s_in[op, o, i : i + 1, :] for o in range(n_ea)], axis=1)
+            h, l = pieces(line)
+            spread_h.append(rows_b[...] * h)
+            spread_l.append(rows_b[...] * l)
+        added = folded(
+            times_transposed(jnp.concatenate(spread_h + spread_l, axis=0), lanes[:dz, :])
+        )
+        vu[op + 1] += added.reshape(comps, dx, dy, dz)
+
+    def yz_apply(op):
         z_low, z_high = z_in[op, 0], z_in[op, 1]
         for i in range(comps):
             for a in range(dx):
@@ -375,41 +374,28 @@
                     z_h.append(jnp.broadcast_to(z_high[:, g : g + 1], (8, dz)))
                 side = side + jnp.where(lane_b == 0, jnp.concatenate(z_l, axis=0), 0.0)
                 side = side + jnp.where(lane_b == dz - 1, jnp.concatenate(z_h, axis=0), 0.0)
-                if a == 0:
-                    side = side + x_in[op, 0, i]
-                if a == dx - 1:
-                    side = side + x_in[op, 1, i]
                 vu[op + 1, i, a] -= side
 
-    def cells_step(op):
-        spread_h, spread_l = [], []
-        for i in range(comps):
-            line = jnp.concatenate([s_in[op, o, i : i + 1, :] for o in range(n_ea)], axis=1)
-            h, l = pieces(line)
-            spread_h.append(rows_b[...] * h)
-            spread_l.append(rows_b[...] * l)
-        added = folded(
-            jnp.dot(
-                jnp.concatenate(spread_h + spread_l, axis=0), lanes_t[...],
-                preferred_element_type=F32,
-            )
-        )
-        vu[op + 1] += added.reshape(comps, dx, dy, dz)
-
-    def last_moment(op, row):
-        x_low = x_in[op, 0] * vu[op, :, 0]
-        x_high = x_in[op, 1] * vu[op, :, dx - 1]
-        side = jnp.sum((x_low + x_high).reshape(comps * dy, dz), axis=0, keepdims=True)
+    def x_apply(op):
+        vu[op + 1, :, 0] -= x_in[op, 0]
+        vu[op + 1, :, dx - 1] -= x_in[op, 1]
+
+    def near_moment(op):
         y = y_in[op, 0] * vu[op, :, :, 0:1] + y_in[op, 1] * vu[op, :, :, dy - 1 : dy]
-        side = side + jnp.sum(y.reshape(comps * dx, dz), axis=0, keepdims=True)
         z = z_out[op, 1] * z_in[op, 0] + z_out[op, 0] * z_in[op, 1]
-        side = side + jnp.sum(z, axis=0, keepdims=True)
+        side = jnp.sum(y.reshape(comps * dx, dz), axis=0, keepdims=True)
+        return side + jnp.sum(z, axis=0, keepdims=True)
+
+    def slot_moment(op):
         cross = None
         for o in range(n_ea):
-            term = p_out[op, o] * s_in[op, o]
+            term = p_in[op, o] * s_out[op, o]
             cross = term if cross is None else cross + term
-        cross = jnp.sum(cross, axis=0, keepdims=True)
-        return row - side + 2.0 * cross
+        return jnp.sum(cross, axis=0, keepdims=True)
+
+    def far_moment(op):
+        x = x_in[op, 0] * vu[op, :, 0] + x_in[op, 1] * vu[op, :, dx - 1]
+        return jnp.sum(x.reshape(comps * dy, dz), axis=0, keepdims=True)
 
     loads["w"].wait()
     wu[0] = jnp.concatenate([w_first[...], jnp.zeros((epad - ecomp, enb), F32)], axis=0)
@@ -420,7 +406,8 @@
 
     column_send(ids_copy)
     column_send(w_copy)
-    halo_send(0)
+    xy_send(0)
+    z_send(0)
     loads["cell"].wait()
     tile = cell[0]
     tile_row = lax.div(tile, dz)
@@ -434,15 +421,11 @@
         r = jnp.where(iota((per, cap), 0) == tile_row[o : o + 1], 1.0, 0.0)
         rows[:, slabs(o)] = r
         rows_b[:, slabs(o)] = r.astype(BF16)
-    pick_send(0, pick(0))
+    pick_send(0)
     loads["coupling"].wait()
     column_send(coup_copy)
 
-    lane_columns = columns(tile_lane)
     for o in range(n_ea):
-        lanes_t[slabs(o), :] = jnp.where(
-            iota((cap, dz), 1) == lane_columns[:, o : o + 1], 1.0, 0.0
-        ).astype(BF16)
         nodes_mine[o] = jnp.where(
             iota((enb, cap), 0) == ids[0, 0, o : o + 1, :], 1.0, 0.0
         ).astype(BF16)
@@ -471,42 +454,42 @@
     ids_in[ek] = ids[:, 0, pl.ds(ek, 1), :]
     coup_in[ek] = coupling[:, :, block(0)]
     landed(ids_in.at[: n_ea - 1], ids_r.at[0])
-    own_rows = jnp.concatenate([ids_in[o, 0] for o in range(n_ea)], axis=0)
-    node_columns = columns(own_rows)
     for o in range(n_ea):
-        nodes_recv[slabs(o), :] = jnp.where(
-            iota((cap, enb), 1) == node_columns[:, o : o + 1], 1.0, 0.0
+        nodes_t[:, slabs(o)] = jnp.where(
+            iota((enb, cap), 0) == ids_in[o, 0], 1.0, 0.0
         ).astype(BF16)
-        nodes_t[:, slabs(o)] = jnp.where(
-            iota((enb, cap), 0) == own_rows[o : o + 1, :], 1.0, 0.0
-        ).astype(BF16)
-
-    halo_wait(0)
-    halo_apply(0)
-    picked = pick(1)
+    yz_wait(0)
+    yz_apply(0)
     first_sums()
-    pick_send(1, picked)
     cells_step(0)
-    halo_send(1)
+    x_wait(0)
+    x_apply(0)
+    xy_send(1)
     landed(coup_in.at[: n_ea - 1], coup_r.at[0])
     for o in range(n_ea):
         for i in range(comps):
             win[o, i] = masked(coup_in[o, i], ids_in[o, 1])
+    picks_wait(0)
     nodes_step(0)
     sums_send(1)
+    z_send(1)
+    pick_send(1)
     last = ITERS - 1
     for op in range(1, last):
         local(op)
         local_nodes(op)
         moments.append(product(op - 1, op))
         moments.append(product(op, op))
-        halo_wait(op)
-        halo_apply(op)
-        picked = pick(op + 1)
         sums_wait(op)
-        pick_send(op + 1, picked)
         cells_step(op)
-        halo_send(op + 1)
+        yz_wait(op)
+        yz_apply(op)
+        x_wait(op)
+        x_apply(op)
+        xy_send(op + 1)
+        z_send(op + 1)
+        pick_send(op + 1)
+        picks_wait(op)
         nodes_step(op)
         sums_send(op + 1)
 
@@ -518,16 +501,16 @@
     packed = jnp.zeros((1, dz), F32)
     for n, m in enumerate(moments):
         packed = jnp.where(lane_r == n, jnp.sum(m, axis=1, keepdims=True), packed)
-    halo_wait(last)
-    sums_wait(last)
-    row = last_moment(last, row)
-    at = 2 * ITERS - 1
-    packed = jnp.where(lane_r == at, jnp.sum(row, axis=1, keepdims=True), packed)
+    red_out[0, 0:1, :] = packed
+    yz_wait(last)
+    picks_wait(last)
+    row = row - near_moment(last) + 2.0 * slot_moment(last)
+    x_wait(last)
+    red_out[0, 1:2, :] = row - far_moment(last)
 
     for stage, group in enumerate(groups):
         total, me, target = members(group)
         whole = group == AXES
-        red_out[stage] = packed
         for d in range(total - 1):
             dst = red.at[stage, me]
             ends = (red_s.at[stage], red_r.at[stage])
@@ -539,11 +522,13 @@
                 ).start()
             else:
                 remote(red_out.at[stage], dst, *ends, target(d + 1)).start()
-        red[stage, me] = packed
+        red[stage, me] = red_out[stage]
         if stage == 0:
-            halo_apply(last)
+            nodes_step(last)
+            yz_apply(last)
+            x_apply(last)
+            sums_wait(last)
             cells_step(last)
-            nodes_step(last)
             for name, buffer, sem in (("gx", x_in, x_s), ("gy", y_in, y_s), ("ea", z_in, z_s)):
                 by_sides(name, buffer, buffer.at[:, 0], sem.at[0])
             landed(p_in.at[:, : n_ea - 1], p_s.at[0])
@@ -553,20 +538,26 @@
             landed(coup_in.at[: n_ea - 1], coup_s.at[0])
         landed(red.at[stage, : total - 1], red_s.at[stage])
         landed(red.at[stage, : total - 1], red_r.at[stage])
-        packed = jnp.sum(red[stage, :total], axis=0)
-
-    sol, res = cg_coefficients([packed[:, n : n + 1] for n in range(2 * ITERS)])
-    tile = jnp.zeros((1, dz), F32)
+        reduced = jnp.sum(red[stage, :total], axis=0)
+        if stage + 1 < len(groups):
+            red_out[stage + 1] = reduced
+
+    early = [jnp.broadcast_to(reduced[0:1, n : n + 1], (1, dz)) for n in range(2 * ITERS - 1)]
+    final = jnp.broadcast_to(jnp.sum(reduced[1:2], axis=1, keepdims=True), (1, dz))
+    sol, res = galerkin_coefficients(early + [final])
     for n, c in enumerate(sol + res):
-        tile = jnp.where(lane_r == n, c, tile)
-    coefs[...] = tile
+        coefs[n : n + 1, :] = c
 
 
 def combine_kernel(vu, wu, coefs, sol_v, res_v, sol_w, res_w):
     ecomp = sol_w.shape[0]
-    tile = coefs[...]
-    solution = [tile[:, n : n + 1] for n in range(ITERS)]
-    residual = [tile[:, ITERS + n : ITERS + n + 1] for n in range(ITERS + 1)]
+    lane_tiles = sol_w.shape[1] // coefs.shape[1]
+
+    def wider(factor):
+        return jnp.concatenate([factor] * lane_tiles, axis=1)
+
+    solution = [coefs[n : n + 1, :] for n in range(ITERS)]
+    residual = [coefs[ITERS + n : ITERS + n + 1, :] for n in range(ITERS + 1)]
 
     def combine(factors, terms):
         out = factors[0] * terms[0]
@@ -580,8 +571,8 @@
     w_terms = [wu[n] for n in range(ITERS + 1)]
     sol_v[...] = combine(solution, v_terms).reshape(shape)
     res_v[...] = combine(residual, v_terms).reshape(shape)
-    sol_w[...] = combine(solution, w_terms)[:ecomp]
-    res_w[...] = combine(residual, w_terms)[:ecomp]
+    sol_w[...] = combine([wider(f) for f in solution], w_terms)[:ecomp]
+    res_w[...] = combine([wider(f) for f in residual], w_terms)[:ecomp]
 
 
 def body(sizes, *args):
@@ -606,11 +597,9 @@
         vmem((n_ea, comps, epad, cap), F32),
         vmem((ecomp, epad, enb), F32),
         vmem((2 * dz, slots), BF16),
-        vmem((slots, dz), BF16),
         vmem((dx * dy, slots), F32),
         vmem((dx * dy, slots), BF16),
         vmem((n_ea, enb, cap), BF16),
-        vmem((slots, enb), BF16),
         vmem((enb, slots), BF16),
         vmem((dx, dy, dz), F32),
         vmem((n_ea, 2, 1, cap), jnp.int32),
@@ -624,8 +613,8 @@
         vmem((ITERS, 2, 8, dz), F32),
         vmem((ITERS, n_ea, comps, cap), F32),
         vmem((ITERS, n_ea, comps, cap), F32),
-        vmem((len(groups), widest, 1, dz), F32),
-        vmem((len(groups), 1, dz), F32),
+        vmem((len(groups), widest, 2, dz), F32),
+        vmem((len(groups), 2, dz), F32),
         dma((1,)), dma((1,)),
         dma((1,)), dma((1,)),
         dma((1,)), dma((ITERS,)),
@@ -641,7 +630,7 @@
         out_shape=(
             pltpu.VMEM((ITERS + 1,) + load_v.shape, F32),
             pltpu.VMEM((ITERS + 1, epad, enb), F32),
-            pltpu.VMEM((1, dz), F32),
+            pltpu.VMEM((2 * ITERS + 2, dz), F32),
         ),
         in_specs=[pl.BlockSpec(memory_space=pltpu.HBM)] * 9,
         out_specs=[pl.BlockSpec(memory_space=vmem)] * 3,

time: 22 us -> 21.7 us (0.986)
  Pallas kernels: 21.1 us -> 20.8 us
    pallas_call x1, Pallas kernels: 20.4 us -> 20.1 us  [body(): pl.pallas_call(functools.partial(kernel, sizes, groups), out_shape=(pltpu...]
where the time goes in v4:
time: 21.7 us; the launch traced here: 21.4 us
  Pallas kernels  20.8 us (96%)
  between operations  0.64 us (3%)
    pallas_call x1, Pallas kernels, body(): pl.pallas_call(functools.partial(kernel, sizes, groups), out_shape=(pltpu...  20.1 us
    pallas_call x1, Pallas kernels, body(): pl.pallas_call(combine_kernel, out_shape=tuple((jax.ShapeDtypeStruct(like...  0.71 us

profile of v4, /device:TPU:0, one launch (start us, length us, event | category | flops | bytes accessed | tf_op | source)
XLA Modules:
  0.0 21.4 jit_solution(5403259681966218490)
XLA Ops:
  0.6 20.1 %krylov.1 = (f32[4,3,4,16,128]{4,3,2,1,0:T(8,128)S(1)}, f32[4,16,256]{2,1,0:T(8,128)S(1)}, f32[8,128]{1,0:T(8,128)S(1)}) custom-call(f32[3,4,16,128]{3,2,1,0:T(8,128)} %load_v.1, f32[15,256]{1,0:T(8,128)} %load_w.1, f32[4,16,128]{2,1,0:T(8,128)} %shift_h.1, f32[15,256]{1,0:T(8,128)} %diag_h.1, f32[15,15,256]{2,1,0:T(8,128)} %off_h.1, ...), custom_call_target="tpu_custom_call" | custom-call | tf_op jit(solution)/shard_map/krylov/pallas_call | solution.py:628
  20.7 0.7 %combine.1 = (f32[3,4,16,128]{3,2,1,0:T(8,128)}, f32[3,4,16,128]{3,2,1,0:T(8,128)}, f32[15,256]{1,0:T(8,128)}, f32[15,256]{1,0:T(8,128)}) custom-call(f32[4,3,4,16,128]{4,3,2,1,0:T(8,128)S(1)} %get-tuple-element.7.vu, f32[4,16,256]{2,1,0:T(8,128)S(1)} %get-tuple-element.8.wu, f32[8,128]{1,0:T(8,128)S(1)} %get-tuple-element.9.coefs), custom_call_target="tpu_custom_call" | custom-call | tf_op jit(solution)/shard_map/combine/pallas_call | solution.py:644

commit v5 on v4

v5 whole, which is shorter than its diff:
```python
import functools

import jax
import jax.numpy as jnp
from jax import lax
from jax.experimental import pallas as pl
from jax.experimental.pallas import tpu as pltpu
from jax.sharding import PartitionSpec as P

ITERS = 3
CENTRE = 11.5
AXES = ("gx", "gy", "ea")
MESH = pl.DeviceIdType.MESH
F32 = jnp.float32
BF16 = jnp.bfloat16


def pieces(x):
    high = x.astype(BF16)
    return high, (x - high.astype(F32)).astype(BF16)


def stacked(x):
    high, low = pieces(x)
    return jnp.concatenate([high, low], axis=0)


def folded(product):
    half = product.shape[0] // 2
    return product[:half] + product[half:]


def iota(shape, dim):
    return lax.broadcasted_iota(jnp.int32, shape, dim)


def times_transposed(a, b):
    return lax.dot_general(
        a, b, (((1,), (1,)), ((), ())), preferred_element_type=F32
    )


def galerkin_coefficients(moment):
    h = [moment[k + 1] + CENTRE * moment[k] for k in range(2 * ITERS - 1)]
    first = 1.0 / h[0]
    l1, l2 = h[1] * first, h[2] * first
    d1 = h[2] - l1 * h[1]
    e = h[3] - l1 * h[2]
    g1 = moment[1] - l1 * moment[0]
    second = 1.0 / d1
    k = e * second
    d2 = h[4] - l2 * h[2] - k * e
    y2 = (moment[2] - l2 * moment[0] - k * g1) / d2
    y1 = (g1 - e * y2) * second
    y0 = (moment[0] - h[1] * y1 - h[2] * y2) * first
    solution = [y0, y1, y2]
    residual = [
        1.0 - CENTRE * y0, -(y0 + CENTRE * y1), -(y1 + CENTRE * y2), -y2
    ]
    return solution, residual


def kernel(
    sizes, groups,
    load_v, load_w, shift_h, diag_h, off_h, coupling_h, kind_h, cell_h, node_h,
    vu, wu, coefs,
    w_first, shift, diag, off, coupling, cell, ids,
    weights, win, stiff, lanes, rows, rows_b, nodes_mine, nodes_t,
    centre_diag, ids_in, coup_in,
    x_in, y_in, z_in, w_in, p_in, s_in, z_out, p_out, s_out, red, red_out,
    red_s, red_r,
):
    n_gx, n_gy, n_ea = sizes
    comps, dx, dy, dz = load_v.shape
    ecomp, enb = load_w.shape
    epad = wu.shape[1]
    cap = cell.shape[2]
    per = dx * dy
    allrows = comps * per
    groups8 = allrows // 8
    gi, gj, ek = (lax.axis_index(a) for a in AXES)
    own = {"gx": gi, "gy": gj, "ea": ek}
    count = dict(zip(AXES, sizes))

    def members(group):
        total = 1
        for a in group:
            total *= count[a]
        me = 0
        for a in group:
            me = me * count[a] + own[a]

        def target(d):
            flat = lax.rem(me + d, total)
            coords = dict(own)
            for a in reversed(group):
                coords[a] = lax.rem(flat, count[a])
                flat = lax.div(flat, count[a])
            return tuple(coords[a] for a in AXES)

        return total, me, target

    def remote(src, dst, s_sem, r_sem, device):
        return pltpu.make_async_remote_copy(
            src_ref=src, dst_ref=dst, send_sem=s_sem, recv_sem=r_sem,
            device_id=device, device_id_type=MESH,
        )

    def landed(ref, sem):
        pltpu.make_async_copy(ref, ref, sem).wait()

    def red_start(stage, group):
        total, me, target = members(group)
        for d in range(total - 1):
            dst = red.at[stage, me]
            ends = (red_s.at[stage], red_r.at[stage])
            if group == AXES:
                pltpu.make_async_remote_copy(
                    src_ref=red_out.at[stage], dst_ref=dst, send_sem=ends[0], recv_sem=ends[1],
                    device_id=d + jnp.where(me <= d, 1, 0),
                    device_id_type=pl.DeviceIdType.LOGICAL,
                ).start()
            else:
                remote(red_out.at[stage], dst, *ends, target(d + 1)).start()
        red[stage, me] = red_out[stage]

    def steps(
        load_s, ids_s, ids_r, coup_s, coup_r, x_s, x_r, y_s, y_r, z_s, z_r,
        w_s, w_r, p_s, p_r, s_s, s_r,
    ):
        has = {
            ("gx", 1): gi < n_gx - 1, ("gx", -1): gi > 0,
            ("gy", 1): gj < n_gy - 1, ("gy", -1): gj > 0,
            ("ea", 1): ek < n_ea - 1, ("ea", -1): ek > 0,
        }
        beside = {
            ("gx", s): (gi + s, gj, ek) for s in (1, -1)
        } | {("gy", s): (gi, gj + s, ek) for s in (1, -1)} | {
            ("ea", s): (gi, gj, ek + s) for s in (1, -1)
        }
        slot = {1: 0, -1: 1}
        sides = {
            name: jnp.where(has[name, 1], 1, 0) + jnp.where(has[name, -1], 1, 0) for name in AXES
        }


        barrier = pltpu.get_barrier_semaphore()
        wide = n_gx - 1 > ITERS
        expected = 0
        for group in groups if wide else (("gy", "ea"),):
            total, _, target = members(group)
            for d in range(1, total):
                pl.semaphore_signal(barrier, inc=1, device_id=target(d), device_id_type=MESH)
            expected += total - 1
        if not wide:
            for s in (1, -1):
                @pl.when(has["gx", s])
                def _():
                    pl.semaphore_signal(
                        barrier, inc=1, device_id=beside["gx", s], device_id_type=MESH
                    )
                expected = expected + jnp.where(has["gx", s], 1, 0)

        loads = {}
        for at, (name, src, dst) in enumerate((
            ("w", load_w, w_first), ("node", node_h, ids.at[0]), ("kind", kind_h, ids.at[1]),
            ("v", load_v, vu.at[0]), ("cell", cell_h, cell), ("coupling", coupling_h, coupling),
            ("shift", shift_h, shift), ("off", off_h, off), ("diag", diag_h, diag),
        )):
            at = 1 if name == "kind" else at
            loads[name] = pltpu.make_async_copy(src, dst, load_s.at[at])
            loads[name].start()

        for s in (1, -1):
            for name, buffer in (("gx", x_in), ("gy", y_in), ("ea", z_in)):
                @pl.when(jnp.logical_not(has[name, -s]))
                def _():
                    for op in range(ITERS):
                        buffer[op, slot[s]] = jnp.zeros(buffer.shape[2:], F32)

        def partner(d):
            return lax.rem(ek + d, n_ea)

        def x_copy(op, s):
            return remote(
                vu.at[op, :, dx - 1 if s == 1 else 0], x_in.at[op, slot[s]],
                x_s.at[0], x_r.at[op], beside["gx", s],
            )

        def y_copy(op, s):
            edge = dy - 1 if s == 1 else 0
            return remote(
                vu.at[op, :, :, edge : edge + 1, :], y_in.at[op, slot[s]],
                y_s.at[0], y_r.at[op], beside["gy", s],
            )

        def z_copy(op, s):
            return remote(
                z_out.at[op, slot[s]], z_in.at[op, slot[s]],
                z_s.at[0], z_r.at[op], beside["ea", s],
            )

        def column_copy(src, dst, s_sem, r_sem, d):
            return remote(src, dst.at[ek], s_sem, r_sem, (gi, gj, partner(d)))

        def w_copy(d):
            return column_copy(wu.at[0], w_in, w_s.at[0], w_r.at[0], d)

        def p_copy(op, d):
            return column_copy(
                p_out.at[op, partner(d)], p_in.at[op], p_s.at[0], p_r.at[op], d
            )

        def s_copy(op, d):
            return column_copy(
                s_out.at[op, partner(d)], s_in.at[op], s_s.at[0], s_r.at[op], d
            )

        def ids_copy(d):
            return column_copy(
                ids.at[:, 0, pl.ds(partner(d), 1), :], ids_in, ids_s.at[0], ids_r.at[0], d
            )

        def block(d):
            return pl.ds(pl.multiple_of(partner(d) * cap, cap), cap)

        def coup_copy(d):
            return column_copy(
                coupling.at[:, :, block(d)], coup_in, coup_s.at[0], coup_r.at[0], d
            )

        def column_send(copy):
            for d in range(1, n_ea):
                copy(d).start()

        lane_i = iota((8, dz), 1)
        lane_r = iota((1, dz), 1)
        row_i = iota((dy, dz), 0)
        lane_b = iota((dy, dz), 1)

        def slabs(o):
            return slice(o * cap, (o + 1) * cap)

        def xy_send(op):
            for s in (1, -1):
                for name, copy in (("gx", x_copy), ("gy", y_copy)):
                    @pl.when(has[name, s])
                    def _():
                        copy(op, s).start()

        def z_send(op):
            v2 = vu[op].reshape(allrows, dz)
            up = jnp.zeros((8, dz), F32)
            down = jnp.zeros((8, dz), F32)
            for g in range(groups8):
                part = v2[8 * g : 8 * g + 8]
                up = jnp.where(lane_i == g, part[:, dz - 1 : dz], up)
                down = jnp.where(lane_i == g, part[:, 0:1], down)
            z_out[op, 0] = up
            z_out[op, 1] = down
            for s in (1, -1):
                @pl.when(has["ea", s])
                def _():
                    z_copy(op, s).start()

        def by_sides(name, two, one, sem):
            @pl.when(sides[name] == 2)
            def _():
                landed(two, sem)

            @pl.when(sides[name] == 1)
            def _():
                landed(one, sem)

        def x_wait(op):
            by_sides("gx", x_in.at[op], x_in.at[op, 0], x_r.at[op])

        def yz_wait(op):
            by_sides("gy", y_in.at[op], y_in.at[op, 0], y_r.at[op])
            by_sides("ea", z_in.at[op], z_in.at[op, 0], z_r.at[op])

        def pick(op):
            h, l = pieces(vu[op].reshape(allrows, dz))
            seen = jnp.dot(
                jnp.concatenate([h, l], axis=1), lanes[...], preferred_element_type=F32
            )
            return [
                jnp.sum(seen[i * per : (i + 1) * per] * rows[...], axis=0, keepdims=True)
                for i in range(comps)
            ]

        def pick_send(op):
            picked = pick(op)
            for i in range(comps):
                for o in range(n_ea):
                    p_out[op, o, i : i + 1, :] = picked[i][:, slabs(o)]
            column_send(functools.partial(p_copy, op))

        def local(op):
            v4 = vu[op]
            v2 = v4.reshape(allrows, dz)
            zero = jnp.zeros((comps, 1, dy, dz), F32)
            near = jnp.concatenate([zero, v4[:, : dx - 1]], axis=1) + jnp.concatenate(
                [v4[:, 1:], zero], axis=1
            )
            near = near.reshape(allrows, dz)
            lane_all = iota((allrows, dz), 1)
            row_all = lax.rem(iota((allrows, dz), 0), dy)
            near = near + jnp.where(lane_all == 0, 0.0, pltpu.roll(v2, 1, 1))
            near = near + jnp.where(lane_all == dz - 1, 0.0, pltpu.roll(v2, dz - 1, 1))
            near = near + jnp.where(row_all == 0, 0.0, pltpu.roll(v2, 1, 0))
            near = near + jnp.where(row_all == dy - 1, 0.0, pltpu.roll(v2, allrows - 1, 0))
            vu[op + 1] = centre_diag[...][None] * v4 - near.reshape(v4.shape)

        def local_nodes(op):
            w = wu[op]
            acc = stiff[0] * w[0:1]
            for p in range(1, ecomp):
                acc = acc + stiff[p] * w[p : p + 1]
            wu[op + 1] = acc

        def product(op_a, op_b):
            pv = jnp.sum((vu[op_a] * vu[op_b]).reshape(groups8, 8, dz), axis=0)
            pw = jnp.sum(wu[op_a] * wu[op_b], axis=0, keepdims=True)
            total = jnp.sum(pv, axis=0, keepdims=True)
            for b in range(enb // dz):
                total = total + pw[:, b * dz : (b + 1) * dz]
            return total

        def picks_wait(op):
            p_in[op, ek] = p_out[op, ek]
            landed(p_in.at[op, : n_ea - 1], p_r.at[op])

        def nodes_step(op):
            terms = []
            for o in range(n_ea):
                total = None
                for i in range(comps):
                    term = win[o, i] * p_in[op, o, i : i + 1, :]
                    total = term if total is None else total + term
                terms.append(total)
            wu[op + 1] += folded(
                times_transposed(stacked(jnp.concatenate(terms, axis=1)), nodes_t[...])
            )

        def sums_send(op):
            values = folded(jnp.dot(stacked(wu[op]), nodes_t[...], preferred_element_type=F32))
            for o in range(n_ea):
                for i in range(comps):
                    s_out[op, o, i : i + 1, :] = jnp.sum(
                        win[o, i] * values[:, slabs(o)], axis=0, keepdims=True
                    )
            column_send(functools.partial(s_copy, op))

        def first_sums():
            w_in[ek] = wu[0]
            landed(w_in.at[: n_ea - 1], w_r.at[0])
            for o in range(n_ea):
                values = folded(jnp.dot(stacked(w_in[o]), nodes_mine[o], preferred_element_type=F32))
                for i in range(comps):
                    s_in[0, o, i : i + 1, :] = jnp.sum(
                        weights[o, i] * values, axis=0, keepdims=True
                    )

        def sums_wait(op):
            s_in[op, ek] = s_out[op, ek]
            landed(s_in.at[op, : n_ea - 1], s_r.at[op])

        def cells_step(op):
            spread_h, spread_l = [], []
            for i in range(comps):
                line = jnp.concatenate([s_in[op, o, i : i + 1, :] for o in range(n_ea)], axis=1)
                h, l = pieces(line)
                spread_h.append(rows_b[...] * h)
                spread_l.append(rows_b[...] * l)
            added = folded(
                times_transposed(jnp.concatenate(spread_h + spread_l, axis=0), lanes[:dz, :])
            )
            vu[op + 1] += added.reshape(comps, dx, dy, dz)

        def yz_apply(op):
            z_low, z_high = z_in[op, 0], z_in[op, 1]
            for i in range(comps):
                for a in range(dx):
                    at = i * dx + a
                    side = jnp.where(row_i == 0, y_in[op, 0, i, a], 0.0)
                    side = side + jnp.where(row_i == dy - 1, y_in[op, 1, i, a], 0.0)
                    z_l, z_h = [], []
                    for b in range(dy // 8):
                        g = at * (dy // 8) + b
                        z_l.append(jnp.broadcast_to(z_low[:, g : g + 1], (8, dz)))
                        z_h.append(jnp.broadcast_to(z_high[:, g : g + 1], (8, dz)))
                    side = side + jnp.where(lane_b == 0, jnp.concatenate(z_l, axis=0), 0.0)
                    side = side + jnp.where(lane_b == dz - 1, jnp.concatenate(z_h, axis=0), 0.0)
                    vu[op + 1, i, a] -= side

        def x_apply(op):
            vu[op + 1, :, 0] -= x_in[op, 0]
            vu[op + 1, :, dx - 1] -= x_in[op, 1]

        def near_moment(op):
            y = y_in[op, 0] * vu[op, :, :, 0:1] + y_in[op, 1] * vu[op, :, :, dy - 1 : dy]
            z = z_out[op, 1] * z_in[op, 0] + z_out[op, 0] * z_in[op, 1]
            side = jnp.sum(y.reshape(comps * dx, dz), axis=0, keepdims=True)
            return side + jnp.sum(z, axis=0, keepdims=True)

        def slot_moment(op):
            cross = None
            for o in range(n_ea):
                term = p_in[op, o] * s_out[op, o]
                cross = term if cross is None else cross + term
            return jnp.sum(cross, axis=0, keepdims=True)

        def far_moment(op):
            x = x_in[op, 0] * vu[op, :, 0] + x_in[op, 1] * vu[op, :, dx - 1]
            return jnp.sum(x.reshape(comps * dy, dz), axis=0, keepdims=True)

        loads["w"].wait()
        wu[0] = jnp.concatenate([w_first[...], jnp.zeros((epad - ecomp, enb), F32)], axis=0)
        landed(ids, load_s.at[1])
        loads["v"].wait()

        pl.semaphore_wait(barrier, expected)

        column_send(ids_copy)
        column_send(w_copy)
        xy_send(0)
        z_send(0)
        loads["coupling"].wait()
        column_send(coup_copy)
        loads["cell"].wait()
        tile = cell[0]
        tile_row = lax.div(tile, dz)
        tile_lane = tile - tile_row * dz
        for o in range(n_ea):
            hot = jnp.where(
                iota((dz, cap), 0) == tile_lane[o : o + 1], 1.0, 0.0
            ).astype(BF16)
            lanes[:dz, slabs(o)] = hot
            lanes[dz:, slabs(o)] = hot
            r = jnp.where(iota((per, cap), 0) == tile_row[o : o + 1], 1.0, 0.0)
            rows[:, slabs(o)] = r
            rows_b[:, slabs(o)] = r.astype(BF16)
        pick_send(0)

        for o in range(n_ea):
            nodes_mine[o] = jnp.where(
                iota((enb, cap), 0) == ids[0, 0, o : o + 1, :], 1.0, 0.0
            ).astype(BF16)
        no_row = jnp.zeros((epad - ecomp, cap), F32)

        def masked(raw, k):
            heavi = jnp.where(k >= 1, 1.0, 0.0)
            tip = jnp.where(k == 2, 1.0, 0.0)
            mask = jnp.where(iota((ecomp, cap), 0) < 3, heavi, tip)
            return jnp.concatenate([raw * mask, no_row], axis=0)

        for o in range(n_ea):
            for i in range(comps):
                weights[o, i] = masked(coupling[i, :, slabs(o)], ids[1, 0, o : o + 1, :])
        loads["shift"].wait()
        centre_diag[...] = shift[...] + (6.0 - CENTRE)
        local(0)
        loads["off"].wait()
        loads["diag"].wait()
        for p in range(ecomp):
            whole = 0.5 * (off[p] + off[:, p, :])
            whole = jnp.where(iota((ecomp, enb), 0) == p, diag[p : p + 1, :] - CENTRE, whole)
            stiff[p] = jnp.concatenate([whole, jnp.zeros((epad - ecomp, enb), F32)], axis=0)
        local_nodes(0)
        moments = [product(0, 0)]
        ids_in[ek] = ids[:, 0, pl.ds(ek, 1), :]
        coup_in[ek] = coupling[:, :, block(0)]
        landed(ids_in.at[: n_ea - 1], ids_r.at[0])
        for o in range(n_ea):
            nodes_t[:, slabs(o)] = jnp.where(
                iota((enb, cap), 0) == ids_in[o, 0], 1.0, 0.0
            ).astype(BF16)
        yz_wait(0)
        yz_apply(0)
        first_sums()
        cells_step(0)
        x_wait(0)
        x_apply(0)
        xy_send(1)
        landed(coup_in.at[: n_ea - 1], coup_r.at[0])
        for o in range(n_ea):
            for i in range(comps):
                win[o, i] = masked(coup_in[o, i], ids_in[o, 1])
        picks_wait(0)
        nodes_step(0)
        sums_send(1)
        pick_send(1)
        z_send(1)
        last = ITERS - 1
        for op in range(1, last):
            local(op)
            local_nodes(op)
            moments.append(product(op - 1, op))
            moments.append(product(op, op))
            yz_wait(op)
            yz_apply(op)
            sums_wait(op)
            cells_step(op)
            x_wait(op)
            x_apply(op)
            xy_send(op + 1)
            pick_send(op + 1)
            z_send(op + 1)
            picks_wait(op)
            nodes_step(op)
            sums_send(op + 1)

        local(last)
        local_nodes(last)
        moments.append(product(last - 1, last))
        moments.append(product(last, last))
        row = product(last, last + 1)
        packed = jnp.zeros((1, dz), F32)
        for n, m in enumerate(moments):
            packed = jnp.where(lane_r == n, jnp.sum(m, axis=1, keepdims=True), packed)
        red_out[0, 0:1, :] = packed
        yz_wait(last)
        picks_wait(last)
        row = row - near_moment(last) + 2.0 * slot_moment(last)
        x_wait(last)
        red_out[0, 1:2, :] = row - far_moment(last)

        red_start(0, groups[0])
        nodes_step(last)
        yz_apply(last)
        x_apply(last)
        sums_wait(last)
        cells_step(last)
        for name, buffer, sem in (("gx", x_in, x_s), ("gy", y_in, y_s), ("ea", z_in, z_s)):
            by_sides(name, buffer, buffer.at[:, 0], sem.at[0])
        landed(p_in.at[:, : n_ea - 1], p_s.at[0])
        landed(s_in.at[1:, : n_ea - 1], s_s.at[0])
        landed(w_in.at[: n_ea - 1], w_s.at[0])
        landed(ids_in.at[: n_ea - 1], ids_s.at[0])
        landed(coup_in.at[: n_ea - 1], coup_s.at[0])

    dma = pltpu.SemaphoreType.DMA
    one, each = dma((1,)), dma((ITERS,))
    pl.run_scoped(
        steps, dma((9,)), one, one, one, one, one, each, one, each, one, each,
        one, one, one, each, one, each,
    )

    for stage, group in enumerate(groups):
        total = members(group)[0]
        if stage > 0:
            red_out[stage] = reduced
            red_start(stage, group)
        landed(red.at[stage, : total - 1], red_s.at[stage])
        landed(red.at[stage, : total - 1], red_r.at[stage])
        reduced = jnp.sum(red[stage, :total], axis=0)

    early = [jnp.broadcast_to(reduced[0:1, n : n + 1], (1, dz)) for n in range(2 * ITERS - 1)]
    final = jnp.broadcast_to(jnp.sum(reduced[1:2], axis=1, keepdims=True), (1, dz))
    sol, res = galerkin_coefficients(early + [final])
    for n, c in enumerate(sol + res):
        coefs[n : n + 1, :] = c


def combine_kernel(vu, wu, coefs, sol_v, res_v, sol_w, res_w):
    ecomp = sol_w.shape[0]
    lane_tiles = sol_w.shape[1] // coefs.shape[1]

    def wider(factor):
        return jnp.concatenate([factor] * lane_tiles, axis=1)

    solution = [coefs[n : n + 1, :] for n in range(ITERS)]
    residual = [coefs[ITERS + n : ITERS + n + 1, :] for n in range(ITERS + 1)]

    def combine(factors, terms):
        out = factors[0] * terms[0]
        for f, t in zip(factors[1:], terms[1:]):
            out = out + f * t
        return out

    shape = sol_v.shape
    flat = (shape[0] * shape[1] * shape[2], shape[3])
    v_terms = [vu[n].reshape(flat) for n in range(ITERS + 1)]
    w_terms = [wu[n] for n in range(ITERS + 1)]
    sol_v[...] = combine(solution, v_terms).reshape(shape)
    res_v[...] = combine(residual, v_terms).reshape(shape)
    sol_w[...] = combine([wider(f) for f in solution], w_terms)[:ecomp]
    res_w[...] = combine([wider(f) for f in residual], w_terms)[:ecomp]


def body(sizes, *args):
    load_v, load_w, shift, diag, off, coupling, kind, cell, node = args
    n_ea = sizes[2]
    total = sizes[0] * sizes[1] * sizes[2]
    groups = (AXES,) if total <= 64 else (("gx",), ("gy", "ea"))
    widest = total if total <= 64 else max(sizes[0], sizes[1] * sizes[2])
    comps, dx, dy, dz = load_v.shape
    ecomp, enb = load_w.shape
    cap = node.shape[2]
    vmem = pltpu.VMEM
    dma = pltpu.SemaphoreType.DMA
    epad = -(-ecomp // 16) * 16
    slots = n_ea * cap
    scratch = [
        vmem(load_w.shape, F32), vmem(shift.shape, F32), vmem(diag.shape, F32),
        vmem(off.shape, F32), vmem(coupling.shape, F32),
        vmem(cell.shape, jnp.int32), vmem((2,) + node.shape, jnp.int32),
        vmem((n_ea, comps, epad, cap), F32),
        vmem((n_ea, comps, epad, cap), F32),
        vmem((ecomp, epad, enb), F32),
        vmem((2 * dz, slots), BF16),
        vmem((dx * dy, slots), F32),
        vmem((dx * dy, slots), BF16),
        vmem((n_ea, enb, cap), BF16),
        vmem((enb, slots), BF16),
        vmem((dx, dy, dz), F32),
        vmem((n_ea, 2, 1, cap), jnp.int32),
        vmem((n_ea, comps, ecomp, cap), F32),
        vmem((ITERS, 2, comps, dy, dz), F32),
        vmem((ITERS, 2, comps, dx, 1, dz), F32),
        vmem((ITERS, 2, 8, dz), F32),
        vmem((n_ea, epad, enb), F32),
        vmem((ITERS, n_ea, comps, cap), F32),
        vmem((ITERS, n_ea, comps, cap), F32),
        vmem((ITERS, 2, 8, dz), F32),
        vmem((ITERS, n_ea, comps, cap), F32),
        vmem((ITERS, n_ea, comps, cap), F32),
        vmem((len(groups), widest, 2, dz), F32),
        vmem((len(groups), 2, dz), F32),
        dma((len(groups),)), dma((len(groups),)),
    ]
    basis = pl.pallas_call(
        functools.partial(kernel, sizes, groups),
        out_shape=(
            pltpu.VMEM((ITERS + 1,) + load_v.shape, F32),
            pltpu.VMEM((ITERS + 1, epad, enb), F32),
            pltpu.VMEM((2 * ITERS + 2, dz), F32),
        ),
        in_specs=[pl.BlockSpec(memory_space=pltpu.HBM)] * 9,
        out_specs=[pl.BlockSpec(memory_space=vmem)] * 3,
        scratch_shapes=scratch,
        compiler_params=pltpu.CompilerParams(
            collective_id=0, has_side_effects=True
        ),
        name="krylov",
    )(*args)
    return tuple(
        pl.pallas_call(
            combine_kernel,
            out_shape=tuple(
                jax.ShapeDtypeStruct(like.shape, F32)
                for like in (load_v, load_v, load_w, load_w)
            ),
            in_specs=[pl.BlockSpec(memory_space=vmem)] * 3,
            out_specs=[pl.BlockSpec(memory_space=vmem)] * 4,
            compiler_params=pltpu.CompilerParams(vmem_limit_bytes=8 << 20),
            name="combine",
        )(*basis)
    )


def solution(mesh):
    column = ("gx", "gy", "ea")
    placed = (
        P(None, "gx", "gy", "ea"),
        P(None, column),
        P("gx", "gy", "ea"),
        P(None, column),
        P(None, None, column),
        P(None, None, column),
        P(column, None, None),
        P(column, None, None),
        P(column, None, None),
    )
    return jax.shard_map(
        functools.partial(body, tuple(mesh.shape[a] for a in AXES)),
        mesh=mesh,
        in_specs=placed,
        out_specs=(
            P(None, "gx", "gy", "ea"),
            P(None, "gx", "gy", "ea"),
            P(None, column),
            P(None, column),
        ),
        check_vma=False,
    )
```

time: 21.7 us -> 21.3 us (0.982)
  Pallas kernels: 20.8 us -> 20.4 us
    pallas_call x1, Pallas kernels: 20.1 us -> 19.7 us  [body(): pl.pallas_call(functools.partial(kernel, sizes, groups), out_shape=(pltpu...]
where the time goes in v5:
time: 21.3 us; the launch traced here: 21.1 us
  Pallas kernels  20.4 us (96%)
  between operations  0.64 us (3%)
    pallas_call x1, Pallas kernels, body(): pl.pallas_call(functools.partial(kernel, sizes, groups), out_shape=(pltpu...  19.7 us
    pallas_call x1, Pallas kernels, body(): pl.pallas_call(combine_kernel, out_shape=tuple((jax.ShapeDtypeStruct(like...  0.71 us

profile of v5, /device:TPU:0, one launch (start us, length us, event | category | flops | bytes accessed | tf_op | source)
XLA Modules:
  0.0 21.1 jit_solution(6087284842961634198)
XLA Ops:
  0.6 19.7 %krylov.1 = (f32[4,3,4,16,128]{4,3,2,1,0:T(8,128)S(1)}, f32[4,16,256]{2,1,0:T(8,128)S(1)}, f32[8,128]{1,0:T(8,128)S(1)}) custom-call(f32[3,4,16,128]{3,2,1,0:T(8,128)} %load_v.1, f32[15,256]{1,0:T(8,128)} %load_w.1, f32[4,16,128]{2,1,0:T(8,128)} %shift_h.1, f32[15,256]{1,0:T(8,128)} %diag_h.1, f32[15,15,256]{2,1,0:T(8,128)} %off_h.1, ...), custom_call_target="tpu_custom_call" | custom-call | tf_op jit(solution)/shard_map/krylov/pallas_call | solution.py:633
  20.3 0.7 %combine.1 = (f32[3,4,16,128]{3,2,1,0:T(8,128)}, f32[3,4,16,128]{3,2,1,0:T(8,128)}, f32[15,256]{1,0:T(8,128)}, f32[15,256]{1,0:T(8,128)}) custom-call(f32[4,3,4,16,128]{4,3,2,1,0:T(8,128)S(1)} %get-tuple-element.7.vu, f32[4,16,256]{2,1,0:T(8,128)S(1)} %get-tuple-element.8.wu, f32[8,128]{1,0:T(8,128)S(1)} %get-tuple-element.9.coefs), custom_call_target="tpu_custom_call" | custom-call | tf_op jit(solution)/shard_map/combine/pallas_call | solution.py:649

commit v6 on v5

--- a/solution.py
+++ b/solution.py
@@ -65,7 +65,7 @@
     load_v, load_w, shift_h, diag_h, off_h, coupling_h, kind_h, cell_h, node_h,
     vu, wu, coefs,
     w_first, shift, diag, off, coupling, cell, ids,
-    weights, win, stiff, lanes, rows, rows_b, nodes_mine, nodes_t,
+    weights, win, stiff, lanes, rows, rows_b, nodes_mine, nodes_t, overlap,
     centre_diag, ids_in, coup_in,
     x_in, y_in, z_in, w_in, p_in, s_in, z_out, p_out, s_out, red, red_out,
     red_s, red_r,
@@ -331,7 +331,7 @@
             p_in[op, ek] = p_out[op, ek]
             landed(p_in.at[op, : n_ea - 1], p_r.at[op])
 
-        def nodes_step(op):
+        def slot_terms(op):
             terms = []
             for o in range(n_ea):
                 total = None
@@ -339,12 +339,15 @@
                     term = win[o, i] * p_in[op, o, i : i + 1, :]
                     total = term if total is None else total + term
                 terms.append(total)
-            wu[op + 1] += folded(
-                times_transposed(stacked(jnp.concatenate(terms, axis=1)), nodes_t[...])
-            )
-
-        def sums_send(op):
-            values = folded(jnp.dot(stacked(wu[op]), nodes_t[...], preferred_element_type=F32))
+            return stacked(jnp.concatenate(terms, axis=1))
+
+        def nodes_step(op, terms):
+            wu[op + 1] += folded(times_transposed(terms, nodes_t[...]))
+
+        def at_slots(op):
+            return folded(jnp.dot(stacked(wu[op]), nodes_t[...], preferred_element_type=F32))
+
+        def sums_send(op, values):
             for o in range(n_ea):
                 for i in range(comps):
                     s_out[op, o, i : i + 1, :] = jnp.sum(
@@ -418,16 +421,14 @@
         loads["w"].wait()
         wu[0] = jnp.concatenate([w_first[...], jnp.zeros((epad - ecomp, enb), F32)], axis=0)
         landed(ids, load_s.at[1])
-        loads["v"].wait()
 
         pl.semaphore_wait(barrier, expected)
 
         column_send(ids_copy)
         column_send(w_copy)
+        loads["v"].wait()
         xy_send(0)
         z_send(0)
-        loads["coupling"].wait()
-        column_send(coup_copy)
         loads["cell"].wait()
         tile = cell[0]
         tile_row = lax.div(tile, dz)
@@ -442,6 +443,8 @@
             rows[:, slabs(o)] = r
             rows_b[:, slabs(o)] = r.astype(BF16)
         pick_send(0)
+        loads["coupling"].wait()
+        column_send(coup_copy)
 
         for o in range(n_ea):
             nodes_mine[o] = jnp.where(
@@ -476,22 +479,38 @@
             nodes_t[:, slabs(o)] = jnp.where(
                 iota((enb, cap), 0) == ids_in[o, 0], 1.0, 0.0
             ).astype(BF16)
+        own_rows = jnp.concatenate([ids_in[o, 0] for o in range(n_ea)], axis=0)
+        own_columns = jnp.transpose(
+            jnp.concatenate(
+                [own_rows.astype(F32), jnp.zeros((cap - n_ea, cap), F32)], axis=0
+            )
+        ).astype(jnp.int32)
         yz_wait(0)
         yz_apply(0)
+        for a in range(n_ea):
+            for b in range(n_ea):
+                overlap[slabs(a), slabs(b)] = jnp.where(
+                    own_columns[:, a : a + 1] == own_rows[b : b + 1, :], 1.0, 0.0
+                ).astype(BF16)
         first_sums()
         cells_step(0)
         x_wait(0)
         x_apply(0)
         xy_send(1)
+        pick_send(1)
+        values = at_slots(1)
         landed(coup_in.at[: n_ea - 1], coup_r.at[0])
         for o in range(n_ea):
             for i in range(comps):
                 win[o, i] = masked(coup_in[o, i], ids_in[o, 1])
         picks_wait(0)
-        nodes_step(0)
-        sums_send(1)
-        pick_send(1)
+        terms = slot_terms(0)
+        values = values + folded(
+            jnp.dot(terms, overlap[...], preferred_element_type=F32)
+        )
+        sums_send(1, values)
         z_send(1)
+        nodes_step(0, terms)
         last = ITERS - 1
         for op in range(1, last):
             local(op)
@@ -508,8 +527,8 @@
             pick_send(op + 1)
             z_send(op + 1)
             picks_wait(op)
-            nodes_step(op)
-            sums_send(op + 1)
+            nodes_step(op, slot_terms(op))
+            sums_send(op + 1, at_slots(op + 1))
 
         local(last)
         local_nodes(last)
@@ -527,7 +546,7 @@
         red_out[0, 1:2, :] = row - far_moment(last)
 
         red_start(0, groups[0])
-        nodes_step(last)
+        nodes_step(last, slot_terms(last))
         yz_apply(last)
         x_apply(last)
         sums_wait(last)
@@ -614,6 +633,7 @@
         vmem((dx * dy, slots), BF16),
         vmem((n_ea, enb, cap), BF16),
         vmem((enb, slots), BF16),
+        vmem((slots, slots), BF16),
         vmem((dx, dy, dz), F32),
         vmem((n_ea, 2, 1, cap), jnp.int32),
         vmem((n_ea, comps, ecomp, cap), F32),

time: 21.3 us -> 21.1 us (level)
  no operation moved by 1% of the time
where the time goes in v6:
time: 21.1 us; the launch traced here: 20.9 us
  Pallas kernels  20.3 us (96%)
  between operations  0.64 us (3%)
    pallas_call x1, Pallas kernels, body(): pl.pallas_call(functools.partial(kernel, sizes, groups), out_shape=(pltpu...  19.6 us
    pallas_call x1, Pallas kernels, body(): pl.pallas_call(combine_kernel, out_shape=tuple((jax.ShapeDtypeStruct(like...  0.71 us

profile of v6, /device:TPU:0, one launch (start us, length us, event | category | flops | bytes accessed | tf_op | source)
XLA Modules:
  0.0 20.9 jit_solution(13592446266928239159)
XLA Ops:
  0.6 19.6 %krylov.1 = (f32[4,3,4,16,128]{4,3,2,1,0:T(8,128)S(1)}, f32[4,16,256]{2,1,0:T(8,128)S(1)}, f32[8,128]{1,0:T(8,128)S(1)}) custom-call(f32[3,4,16,128]{3,2,1,0:T(8,128)} %load_v.1, f32[15,256]{1,0:T(8,128)} %load_w.1, f32[4,16,128]{2,1,0:T(8,128)} %shift_h.1, f32[15,256]{1,0:T(8,128)} %diag_h.1, f32[15,15,256]{2,1,0:T(8,128)} %off_h.1, ...), custom_call_target="tpu_custom_call" | custom-call | tf_op jit(solution)/shard_map/krylov/pallas_call | solution.py:653
  20.2 0.7 %combine.1 = (f32[3,4,16,128]{3,2,1,0:T(8,128)}, f32[3,4,16,128]{3,2,1,0:T(8,128)}, f32[15,256]{1,0:T(8,128)}, f32[15,256]{1,0:T(8,128)}) custom-call(f32[4,3,4,16,128]{4,3,2,1,0:T(8,128)S(1)} %get-tuple-element.7.vu, f32[4,16,256]{2,1,0:T(8,128)S(1)} %get-tuple-element.8.wu, f32[8,128]{1,0:T(8,128)S(1)} %get-tuple-element.9.coefs), custom_call_target="tpu_custom_call" | custom-call | tf_op jit(solution)/shard_map/combine/pallas_call | solution.py:669

commit v7 on v6

--- a/solution.py
+++ b/solution.py
@@ -76,6 +76,7 @@
     epad = wu.shape[1]
     cap = cell.shape[2]
     per = dx * dy
+    half = per // 2
     allrows = comps * per
     groups8 = allrows // 8
     gi, gj, ek = (lax.axis_index(a) for a in AXES)
@@ -280,12 +281,20 @@
             by_sides("ea", z_in.at[op], z_in.at[op, 0], z_r.at[op])
 
         def pick(op):
-            h, l = pieces(vu[op].reshape(allrows, dz))
-            seen = jnp.dot(
-                jnp.concatenate([h, l], axis=1), lanes[...], preferred_element_type=F32
+            v3 = vu[op].reshape(comps, per, dz)
+            folds = jnp.concatenate(
+                [
+                    jnp.concatenate([v3[i, :half], v3[i, half:]], axis=1)
+                    for i in range(comps)
+                ],
+                axis=0,
+            )
+            h, l = pieces(folds)
+            seen = jnp.dot(h, lanes[...], preferred_element_type=F32) + jnp.dot(
+                l, lanes[...], preferred_element_type=F32
             )
             return [
-                jnp.sum(seen[i * per : (i + 1) * per] * rows[...], axis=0, keepdims=True)
+                jnp.sum(seen[i * half : (i + 1) * half] * rows[...], axis=0, keepdims=True)
                 for i in range(comps)
             ]
 
@@ -376,10 +385,15 @@
                 h, l = pieces(line)
                 spread_h.append(rows_b[...] * h)
                 spread_l.append(rows_b[...] * l)
-            added = folded(
-                times_transposed(jnp.concatenate(spread_h + spread_l, axis=0), lanes[:dz, :])
-            )
-            vu[op + 1] += added.reshape(comps, dx, dy, dz)
+            added = times_transposed(
+                jnp.concatenate(spread_h, axis=0), lanes[...]
+            ) + times_transposed(jnp.concatenate(spread_l, axis=0), lanes[...])
+            for i in range(comps):
+                for a in range(dx):
+                    at = a * dy
+                    part = at // half
+                    low = i * half + at - part * half
+                    vu[op + 1, i, a] += added[low : low + dy, part * dz : (part + 1) * dz]
 
         def yz_apply(op):
             z_low, z_high = z_in[op, 0], z_in[op, 1]
@@ -434,12 +448,12 @@
         tile_row = lax.div(tile, dz)
         tile_lane = tile - tile_row * dz
         for o in range(n_ea):
-            hot = jnp.where(
-                iota((dz, cap), 0) == tile_lane[o : o + 1], 1.0, 0.0
+            here = tile_lane[o : o + 1] + jnp.where(tile_row[o : o + 1] >= half, dz, 0)
+            lanes[:, slabs(o)] = jnp.where(
+                iota((2 * dz, cap), 0) == here, 1.0, 0.0
             ).astype(BF16)
-            lanes[:dz, slabs(o)] = hot
-            lanes[dz:, slabs(o)] = hot
-            r = jnp.where(iota((per, cap), 0) == tile_row[o : o + 1], 1.0, 0.0)
+            below = lax.rem(tile_row[o : o + 1], half)
+            r = jnp.where(iota((half, cap), 0) == below, 1.0, 0.0)
             rows[:, slabs(o)] = r
             rows_b[:, slabs(o)] = r.astype(BF16)
         pick_send(0)
@@ -487,17 +501,16 @@
         ).astype(jnp.int32)
         yz_wait(0)
         yz_apply(0)
+        first_sums()
+        cells_step(0)
+        x_wait(0)
+        x_apply(0)
+        xy_send(1)
         for a in range(n_ea):
             for b in range(n_ea):
                 overlap[slabs(a), slabs(b)] = jnp.where(
                     own_columns[:, a : a + 1] == own_rows[b : b + 1, :], 1.0, 0.0
                 ).astype(BF16)
-        first_sums()
-        cells_step(0)
-        x_wait(0)
-        x_apply(0)
-        xy_send(1)
-        pick_send(1)
         values = at_slots(1)
         landed(coup_in.at[: n_ea - 1], coup_r.at[0])
         for o in range(n_ea):
@@ -510,6 +523,7 @@
         )
         sums_send(1, values)
         z_send(1)
+        pick_send(1)
         nodes_step(0, terms)
         last = ITERS - 1
         for op in range(1, last):
@@ -629,8 +643,8 @@
         vmem((n_ea, comps, epad, cap), F32),
         vmem((ecomp, epad, enb), F32),
         vmem((2 * dz, slots), BF16),
-        vmem((dx * dy, slots), F32),
-        vmem((dx * dy, slots), BF16),
+        vmem((dx * dy // 2, slots), F32),
+        vmem((dx * dy // 2, slots), BF16),
         vmem((n_ea, enb, cap), BF16),
         vmem((enb, slots), BF16),
         vmem((slots, slots), BF16),

time: 21.1 us -> 21.1 us (level)
  no operation moved by 1% of the time
where the time goes in v7:
time: 21.1 us; the launch traced here: 20.9 us
  Pallas kernels  20.3 us (96%)
  between operations  0.64 us (3%)
    pallas_call x1, Pallas kernels, body(): pl.pallas_call(functools.partial(kernel, sizes, groups), out_shape=(pltpu...  19.6 us
    pallas_call x1, Pallas kernels, body(): pl.pallas_call(combine_kernel, out_shape=tuple((jax.ShapeDtypeStruct(like...  0.71 us

profile of v7, /device:TPU:0, one launch (start us, length us, event | category | flops | bytes accessed | tf_op | source)
XLA Modules:
  0.0 20.9 jit_solution(15599788474618664608)
XLA Ops:
  0.6 19.6 %krylov.1 = (f32[4,3,4,16,128]{4,3,2,1,0:T(8,128)S(1)}, f32[4,16,256]{2,1,0:T(8,128)S(1)}, f32[8,128]{1,0:T(8,128)S(1)}) custom-call(f32[3,4,16,128]{3,2,1,0:T(8,128)} %load_v.1, f32[15,256]{1,0:T(8,128)} %load_w.1, f32[4,16,128]{2,1,0:T(8,128)} %shift_h.1, f32[15,256]{1,0:T(8,128)} %diag_h.1, f32[15,15,256]{2,1,0:T(8,128)} %off_h.1, ...), custom_call_target="tpu_custom_call" | custom-call | tf_op jit(solution)/shard_map/krylov/pallas_call | solution.py:667
  20.2 0.7 %combine.1 = (f32[3,4,16,128]{3,2,1,0:T(8,128)}, f32[3,4,16,128]{3,2,1,0:T(8,128)}, f32[15,256]{1,0:T(8,128)}, f32[15,256]{1,0:T(8,128)}) custom-call(f32[4,3,4,16,128]{4,3,2,1,0:T(8,128)S(1)} %get-tuple-element.7.vu, f32[4,16,256]{2,1,0:T(8,128)S(1)} %get-tuple-element.8.wu, f32[8,128]{1,0:T(8,128)S(1)} %get-tuple-element.9.coefs), custom_call_target="tpu_custom_call" | custom-call | tf_op jit(solution)/shard_map/combine/pallas_call | solution.py:683

commit v8 on v7

--- a/solution.py
+++ b/solution.py
@@ -127,7 +127,7 @@
 
     def steps(
         load_s, ids_s, ids_r, coup_s, coup_r, x_s, x_r, y_s, y_r, z_s, z_r,
-        w_s, w_r, p_s, p_r, s_s, s_r,
+        w_s, w_r, p_s, p_r, s_s, s_r, known,
     ):
         has = {
             ("gx", 1): gi < n_gx - 1, ("gx", -1): gi > 0,
@@ -146,21 +146,33 @@
 
 
         barrier = pltpu.get_barrier_semaphore()
-        wide = n_gx - 1 > ITERS
-        expected = 0
-        for group in groups if wide else (("gy", "ea"),):
-            total, _, target = members(group)
-            for d in range(1, total):
-                pl.semaphore_signal(barrier, inc=1, device_id=target(d), device_id_type=MESH)
-            expected += total - 1
-        if not wide:
-            for s in (1, -1):
-                @pl.when(has["gx", s])
-                def _():
+        wide = n_gx + n_gy - 2 + (n_ea > 1) > ITERS + 2
+
+        def greet(sem):
+            for d in range(1, n_ea):
+                pl.semaphore_signal(
+                    sem, inc=1, device_id=(gi, gj, lax.rem(ek + d, n_ea)), device_id_type=MESH
+                )
+            for name in ("gx", "gy"):
+                for s in (1, -1):
+                    @pl.when(has[name, s])
+                    def _():
+                        pl.semaphore_signal(
+                            sem, inc=1, device_id=beside[name, s], device_id_type=MESH
+                        )
+
+        if wide:
+            expected = 0
+            for group in groups:
+                total, _, target = members(group)
+                for d in range(1, total):
                     pl.semaphore_signal(
-                        barrier, inc=1, device_id=beside["gx", s], device_id_type=MESH
+                        barrier, inc=1, device_id=target(d), device_id_type=MESH
                     )
-                expected = expected + jnp.where(has["gx", s], 1, 0)
+                expected += total - 1
+        else:
+            greet(barrier)
+            expected = n_ea - 1 + sides["gx"] + sides["gy"]
 
         loads = {}
         for at, (name, src, dst) in enumerate((
@@ -289,10 +301,7 @@
                 ],
                 axis=0,
             )
-            h, l = pieces(folds)
-            seen = jnp.dot(h, lanes[...], preferred_element_type=F32) + jnp.dot(
-                l, lanes[...], preferred_element_type=F32
-            )
+            seen = folded(jnp.dot(stacked(folds), lanes[...], preferred_element_type=F32))
             return [
                 jnp.sum(seen[i * half : (i + 1) * half] * rows[...], axis=0, keepdims=True)
                 for i in range(comps)
@@ -385,9 +394,9 @@
                 h, l = pieces(line)
                 spread_h.append(rows_b[...] * h)
                 spread_l.append(rows_b[...] * l)
-            added = times_transposed(
-                jnp.concatenate(spread_h, axis=0), lanes[...]
-            ) + times_transposed(jnp.concatenate(spread_l, axis=0), lanes[...])
+            added = folded(
+                times_transposed(jnp.concatenate(spread_h + spread_l, axis=0), lanes[...])
+            )
             for i in range(comps):
                 for a in range(dx):
                     at = a * dy
@@ -440,6 +449,8 @@
 
         column_send(ids_copy)
         column_send(w_copy)
+        if not wide:
+            greet(known.at[0])
         loads["v"].wait()
         xy_send(0)
         z_send(0)
@@ -486,8 +497,20 @@
             stiff[p] = jnp.concatenate([whole, jnp.zeros((epad - ecomp, enb), F32)], axis=0)
         local_nodes(0)
         moments = [product(0, 0)]
+        if not wide:
+            pl.semaphore_wait(known.at[0], expected)
+            greet(known.at[1])
         ids_in[ek] = ids[:, 0, pl.ds(ek, 1), :]
         coup_in[ek] = coupling[:, :, block(0)]
+        yz_wait(0)
+        yz_apply(0)
+        first_sums()
+        cells_step(0)
+        x_wait(0)
+        x_apply(0)
+        if not wide:
+            pl.semaphore_wait(known.at[1], expected)
+        xy_send(1)
         landed(ids_in.at[: n_ea - 1], ids_r.at[0])
         for o in range(n_ea):
             nodes_t[:, slabs(o)] = jnp.where(
@@ -499,13 +522,6 @@
                 [own_rows.astype(F32), jnp.zeros((cap - n_ea, cap), F32)], axis=0
             )
         ).astype(jnp.int32)
-        yz_wait(0)
-        yz_apply(0)
-        first_sums()
-        cells_step(0)
-        x_wait(0)
-        x_apply(0)
-        xy_send(1)
         for a in range(n_ea):
             for b in range(n_ea):
                 overlap[slabs(a), slabs(b)] = jnp.where(
@@ -577,7 +593,7 @@
     one, each = dma((1,)), dma((ITERS,))
     pl.run_scoped(
         steps, dma((9,)), one, one, one, one, one, each, one, each, one, each,
-        one, one, one, each, one, each,
+        one, one, one, each, one, each, pltpu.SemaphoreType.REGULAR((2,)),
     )
 
     for stage, group in enumerate(groups):

time: 21.1 us -> 21 us (level)
  no operation moved by 1% of the time
where the time goes in v8:
time: 21 us; the launch traced here: 20.8 us
  Pallas kernels  20.1 us (96%)
  between operations  0.64 us (3%)
    pallas_call x1, Pallas kernels, body(): pl.pallas_call(functools.partial(kernel, sizes, groups), out_shape=(pltpu...  19.4 us
    pallas_call x1, Pallas kernels, body(): pl.pallas_call(combine_kernel, out_shape=tuple((jax.ShapeDtypeStruct(like...  0.71 us

profile of v8, /device:TPU:0, one launch (start us, length us, event | category | flops | bytes accessed | tf_op | source)
XLA Modules:
  0.0 20.8 jit_solution(2041676820998923651)
XLA Ops:
  0.6 19.4 %krylov.1 = (f32[4,3,4,16,128]{4,3,2,1,0:T(8,128)S(1)}, f32[4,16,256]{2,1,0:T(8,128)S(1)}, f32[8,128]{1,0:T(8,128)S(1)}) custom-call(f32[3,4,16,128]{3,2,1,0:T(8,128)} %load_v.1, f32[15,256]{1,0:T(8,128)} %load_w.1, f32[4,16,128]{2,1,0:T(8,128)} %shift_h.1, f32[15,256]{1,0:T(8,128)} %diag_h.1, f32[15,15,256]{2,1,0:T(8,128)} %off_h.1, ...), custom_call_target="tpu_custom_call" | custom-call | tf_op jit(solution)/shard_map/krylov/pallas_call | solution.py:683
  20.1 0.7 %combine.1 = (f32[3,4,16,128]{3,2,1,0:T(8,128)}, f32[3,4,16,128]{3,2,1,0:T(8,128)}, f32[15,256]{1,0:T(8,128)}, f32[15,256]{1,0:T(8,128)}) custom-call(f32[4,3,4,16,128]{4,3,2,1,0:T(8,128)S(1)} %get-tuple-element.7.vu, f32[4,16,256]{2,1,0:T(8,128)S(1)} %get-tuple-element.8.wu, f32[8,128]{1,0:T(8,128)S(1)} %get-tuple-element.9.coefs), custom_call_target="tpu_custom_call" | custom-call | tf_op jit(solution)/shard_map/combine/pallas_call | solution.py:699

commit v9 on v8

--- a/solution.py
+++ b/solution.py
@@ -140,6 +140,7 @@
             ("ea", s): (gi, gj, ek + s) for s in (1, -1)
         }
         slot = {1: 0, -1: 1}
+        last = ITERS - 1
         sides = {
             name: jnp.where(has[name, 1], 1, 0) + jnp.where(has[name, -1], 1, 0) for name in AXES
         }
@@ -194,23 +195,26 @@
         def partner(d):
             return lax.rem(ek + d, n_ea)
 
+        def arrival(op, s):
+            return op + 1 if op == last and s == 1 else op
+
         def x_copy(op, s):
             return remote(
                 vu.at[op, :, dx - 1 if s == 1 else 0], x_in.at[op, slot[s]],
-                x_s.at[0], x_r.at[op], beside["gx", s],
+                x_s.at[0], x_r.at[arrival(op, s)], beside["gx", s],
             )
 
         def y_copy(op, s):
             edge = dy - 1 if s == 1 else 0
             return remote(
                 vu.at[op, :, :, edge : edge + 1, :], y_in.at[op, slot[s]],
-                y_s.at[0], y_r.at[op], beside["gy", s],
+                y_s.at[0], y_r.at[arrival(op, s)], beside["gy", s],
             )
 
         def z_copy(op, s):
             return remote(
                 z_out.at[op, slot[s]], z_in.at[op, slot[s]],
-                z_s.at[0], z_r.at[op], beside["ea", s],
+                z_s.at[0], z_r.at[arrival(op, s)], beside["ea", s],
             )
 
         def column_copy(src, dst, s_sem, r_sem, d):
@@ -292,6 +296,11 @@
             by_sides("gy", y_in.at[op], y_in.at[op, 0], y_r.at[op])
             by_sides("ea", z_in.at[op], z_in.at[op, 0], z_r.at[op])
 
+        def side_wait(name, buffer, sem, s):
+            @pl.when(has[name, -s])
+            def _():
+                landed(buffer.at[last, slot[s]], sem.at[arrival(last, s)])
+
         def pick(op):
             v3 = vu[op].reshape(comps, per, dz)
             folds = jnp.concatenate(
@@ -307,11 +316,13 @@
                 for i in range(comps)
             ]
 
-        def pick_send(op):
-            picked = pick(op)
+        def pick_send(op, picked, added=None):
             for i in range(comps):
                 for o in range(n_ea):
-                    p_out[op, o, i : i + 1, :] = picked[i][:, slabs(o)]
+                    line = picked[i][:, slabs(o)]
+                    if added is not None:
+                        line = line + s_in[added, o, i : i + 1, :]
+                    p_out[op, o, i : i + 1, :] = line
             column_send(functools.partial(p_copy, op))
 
         def local(op):
@@ -425,9 +436,9 @@
             vu[op + 1, :, dx - 1] -= x_in[op, 1]
 
         def near_moment(op):
-            y = y_in[op, 0] * vu[op, :, :, 0:1] + y_in[op, 1] * vu[op, :, :, dy - 1 : dy]
-            z = z_out[op, 1] * z_in[op, 0] + z_out[op, 0] * z_in[op, 1]
+            y = y_in[op, 1] * vu[op, :, :, dy - 1 : dy]
             side = jnp.sum(y.reshape(comps * dx, dz), axis=0, keepdims=True)
+            z = z_out[op, 0] * z_in[op, 1]
             return side + jnp.sum(z, axis=0, keepdims=True)
 
         def slot_moment(op):
@@ -438,7 +449,7 @@
             return jnp.sum(cross, axis=0, keepdims=True)
 
         def far_moment(op):
-            x = x_in[op, 0] * vu[op, :, 0] + x_in[op, 1] * vu[op, :, dx - 1]
+            x = x_in[op, 1] * vu[op, :, dx - 1]
             return jnp.sum(x.reshape(comps * dy, dz), axis=0, keepdims=True)
 
         loads["w"].wait()
@@ -467,7 +478,7 @@
             r = jnp.where(iota((half, cap), 0) == below, 1.0, 0.0)
             rows[:, slabs(o)] = r
             rows_b[:, slabs(o)] = r.astype(BF16)
-        pick_send(0)
+        pick_send(0, pick(0))
         loads["coupling"].wait()
         column_send(coup_copy)
 
@@ -504,6 +515,11 @@
         coup_in[ek] = coupling[:, :, block(0)]
         yz_wait(0)
         yz_apply(0)
+        landed(ids_in.at[: n_ea - 1], ids_r.at[0])
+        for o in range(n_ea):
+            nodes_t[:, slabs(o)] = jnp.where(
+                iota((enb, cap), 0) == ids_in[o, 0], 1.0, 0.0
+            ).astype(BF16)
         first_sums()
         cells_step(0)
         x_wait(0)
@@ -511,11 +527,6 @@
         if not wide:
             pl.semaphore_wait(known.at[1], expected)
         xy_send(1)
-        landed(ids_in.at[: n_ea - 1], ids_r.at[0])
-        for o in range(n_ea):
-            nodes_t[:, slabs(o)] = jnp.where(
-                iota((enb, cap), 0) == ids_in[o, 0], 1.0, 0.0
-            ).astype(BF16)
         own_rows = jnp.concatenate([ids_in[o, 0] for o in range(n_ea)], axis=0)
         own_columns = jnp.transpose(
             jnp.concatenate(
@@ -539,9 +550,8 @@
         )
         sums_send(1, values)
         z_send(1)
-        pick_send(1)
+        pick_send(1, pick(1))
         nodes_step(0, terms)
-        last = ITERS - 1
         for op in range(1, last):
             local(op)
             local_nodes(op)
@@ -549,12 +559,13 @@
             moments.append(product(op, op))
             yz_wait(op)
             yz_apply(op)
-            sums_wait(op)
-            cells_step(op)
             x_wait(op)
             x_apply(op)
+            picked = pick(op + 1)
+            sums_wait(op)
+            pick_send(op + 1, picked, added=op)
+            cells_step(op)
             xy_send(op + 1)
-            pick_send(op + 1)
             z_send(op + 1)
             picks_wait(op)
             nodes_step(op, slot_terms(op))
@@ -569,14 +580,19 @@
         for n, m in enumerate(moments):
             packed = jnp.where(lane_r == n, jnp.sum(m, axis=1, keepdims=True), packed)
         red_out[0, 0:1, :] = packed
-        yz_wait(last)
+        halos = (("ea", z_in, z_r), ("gy", y_in, y_r), ("gx", x_in, x_r))
         picks_wait(last)
-        row = row - near_moment(last) + 2.0 * slot_moment(last)
-        x_wait(last)
-        red_out[0, 1:2, :] = row - far_moment(last)
+        row = row + 2.0 * slot_moment(last)
+        for name, buffer, sem in halos[:2]:
+            side_wait(name, buffer, sem, -1)
+        row = row - 2.0 * near_moment(last)
+        side_wait(*halos[2], -1)
+        red_out[0, 1:2, :] = row - 2.0 * far_moment(last)
 
         red_start(0, groups[0])
         nodes_step(last, slot_terms(last))
+        for name, buffer, sem in halos:
+            side_wait(name, buffer, sem, 1)
         yz_apply(last)
         x_apply(last)
         sums_wait(last)
@@ -590,9 +606,9 @@
         landed(coup_in.at[: n_ea - 1], coup_s.at[0])
 
     dma = pltpu.SemaphoreType.DMA
-    one, each = dma((1,)), dma((ITERS,))
+    one, each, more = dma((1,)), dma((ITERS,)), dma((ITERS + 1,))
     pl.run_scoped(
-        steps, dma((9,)), one, one, one, one, one, each, one, each, one, each,
+        steps, dma((9,)), one, one, one, one, one, more, one, more, one, more,
         one, one, one, each, one, each, pltpu.SemaphoreType.REGULAR((2,)),
     )
 

time: 21 us -> 20.6 us (0.981)
  Pallas kernels: 20.1 us -> 19.7 us
    pallas_call x1, Pallas kernels: 19.4 us -> 19 us  [body(): pl.pallas_call(functools.partial(kernel, sizes, groups), out_shape=(pltpu...]
where the time goes in v9:
time: 20.6 us; the launch traced here: 20.3 us
  Pallas kernels  19.7 us (96%)
  between operations  0.64 us (3%)
    pallas_call x1, Pallas kernels, body(): pl.pallas_call(functools.partial(kernel, sizes, groups), out_shape=(pltpu...  19 us
    pallas_call x1, Pallas kernels, body(): pl.pallas_call(combine_kernel, out_shape=tuple((jax.ShapeDtypeStruct(like...  0.71 us

profile of v9, /device:TPU:0, one launch (start us, length us, event | category | flops | bytes accessed | tf_op | source)
XLA Modules:
  0.0 20.3 jit_solution(17677654871189404672)
XLA Ops:
  0.6 19.0 %krylov.1 = (f32[4,3,4,16,128]{4,3,2,1,0:T(8,128)S(1)}, f32[4,16,256]{2,1,0:T(8,128)S(1)}, f32[8,128]{1,0:T(8,128)S(1)}) custom-call(f32[3,4,16,128]{3,2,1,0:T(8,128)} %load_v.1, f32[15,256]{1,0:T(8,128)} %load_w.1, f32[4,16,128]{2,1,0:T(8,128)} %shift_h.1, f32[15,256]{1,0:T(8,128)} %diag_h.1, f32[15,15,256]{2,1,0:T(8,128)} %off_h.1, ...), custom_call_target="tpu_custom_call" | custom-call | tf_op jit(solution)/shard_map/krylov/pallas_call | solution.py:699
  19.6 0.7 %combine.1 = (f32[3,4,16,128]{3,2,1,0:T(8,128)}, f32[3,4,16,128]{3,2,1,0:T(8,128)}, f32[15,256]{1,0:T(8,128)}, f32[15,256]{1,0:T(8,128)}) custom-call(f32[4,3,4,16,128]{4,3,2,1,0:T(8,128)S(1)} %get-tuple-element.7.vu, f32[4,16,256]{2,1,0:T(8,128)S(1)} %get-tuple-element.8.wu, f32[8,128]{1,0:T(8,128)S(1)} %get-tuple-element.9.coefs), custom_call_target="tpu_custom_call" | custom-call | tf_op jit(solution)/shard_map/combine/pallas_call | solution.py:715

commit v10 on v9

--- a/solution.py
+++ b/solution.py
@@ -516,6 +516,12 @@
         yz_wait(0)
         yz_apply(0)
         landed(ids_in.at[: n_ea - 1], ids_r.at[0])
+        own_rows = jnp.concatenate([ids_in[o, 0] for o in range(n_ea)], axis=0)
+        own_columns = jnp.transpose(
+            jnp.concatenate(
+                [own_rows.astype(F32), jnp.zeros((cap - n_ea, cap), F32)], axis=0
+            )
+        ).astype(jnp.int32)
         for o in range(n_ea):
             nodes_t[:, slabs(o)] = jnp.where(
                 iota((enb, cap), 0) == ids_in[o, 0], 1.0, 0.0
@@ -527,12 +533,6 @@
         if not wide:
             pl.semaphore_wait(known.at[1], expected)
         xy_send(1)
-        own_rows = jnp.concatenate([ids_in[o, 0] for o in range(n_ea)], axis=0)
-        own_columns = jnp.transpose(
-            jnp.concatenate(
-                [own_rows.astype(F32), jnp.zeros((cap - n_ea, cap), F32)], axis=0
-            )
-        ).astype(jnp.int32)
         for a in range(n_ea):
             for b in range(n_ea):
                 overlap[slabs(a), slabs(b)] = jnp.where(
@@ -561,11 +561,23 @@
             yz_apply(op)
             x_wait(op)
             x_apply(op)
-            picked = pick(op + 1)
-            sums_wait(op)
-            pick_send(op + 1, picked, added=op)
-            cells_step(op)
-            xy_send(op + 1)
+            late = ek == n_ea // 2
+
+            @pl.when(late)
+            def _():
+                sums_wait(op)
+                cells_step(op)
+                xy_send(op + 1)
+                pick_send(op + 1, pick(op + 1))
+
+            @pl.when(jnp.logical_not(late))
+            def _():
+                picked = pick(op + 1)
+                sums_wait(op)
+                pick_send(op + 1, picked, added=op)
+                cells_step(op)
+                xy_send(op + 1)
+
             z_send(op + 1)
             picks_wait(op)
             nodes_step(op, slot_terms(op))

time: 20.6 us -> 20.4 us (level)
  no operation moved by 1% of the time
where the time goes in v10:
time: 20.4 us; the launch traced here: 20.1 us
  Pallas kernels  19.5 us (96%)
  between operations  0.64 us (3%)
    pallas_call x1, Pallas kernels, body(): pl.pallas_call(functools.partial(kernel, sizes, groups), out_shape=(pltpu...  18.8 us
    pallas_call x1, Pallas kernels, body(): pl.pallas_call(combine_kernel, out_shape=tuple((jax.ShapeDtypeStruct(like...  0.71 us

profile of v10, /device:TPU:0, one launch (start us, length us, event | category | flops | bytes accessed | tf_op | source)
XLA Modules:
  0.0 20.1 jit_solution(17273960873462534483)
XLA Ops:
  0.6 18.8 %krylov.1 = (f32[4,3,4,16,128]{4,3,2,1,0:T(8,128)S(1)}, f32[4,16,256]{2,1,0:T(8,128)S(1)}, f32[8,128]{1,0:T(8,128)S(1)}) custom-call(f32[3,4,16,128]{3,2,1,0:T(8,128)} %load_v.1, f32[15,256]{1,0:T(8,128)} %load_w.1, f32[4,16,128]{2,1,0:T(8,128)} %shift_h.1, f32[15,256]{1,0:T(8,128)} %diag_h.1, f32[15,15,256]{2,1,0:T(8,128)} %off_h.1, ...), custom_call_target="tpu_custom_call" | custom-call | tf_op jit(solution)/shard_map/krylov/pallas_call | solution.py:711
  19.4 0.7 %combine.1 = (f32[3,4,16,128]{3,2,1,0:T(8,128)}, f32[3,4,16,128]{3,2,1,0:T(8,128)}, f32[15,256]{1,0:T(8,128)}, f32[15,256]{1,0:T(8,128)}) custom-call(f32[4,3,4,16,128]{4,3,2,1,0:T(8,128)S(1)} %get-tuple-element.7.vu, f32[4,16,256]{2,1,0:T(8,128)S(1)} %get-tuple-element.8.wu, f32[8,128]{1,0:T(8,128)S(1)} %get-tuple-element.9.coefs), custom_call_target="tpu_custom_call" | custom-call | tf_op jit(solution)/shard_map/combine/pallas_call | solution.py:727

commit v11 on v10

--- a/solution.py
+++ b/solution.py
@@ -513,31 +513,50 @@
             greet(known.at[1])
         ids_in[ek] = ids[:, 0, pl.ds(ek, 1), :]
         coup_in[ek] = coupling[:, :, block(0)]
-        yz_wait(0)
-        yz_apply(0)
-        landed(ids_in.at[: n_ea - 1], ids_r.at[0])
-        own_rows = jnp.concatenate([ids_in[o, 0] for o in range(n_ea)], axis=0)
-        own_columns = jnp.transpose(
-            jnp.concatenate(
-                [own_rows.astype(F32), jnp.zeros((cap - n_ea, cap), F32)], axis=0
-            )
-        ).astype(jnp.int32)
-        for o in range(n_ea):
-            nodes_t[:, slabs(o)] = jnp.where(
-                iota((enb, cap), 0) == ids_in[o, 0], 1.0, 0.0
-            ).astype(BF16)
-        first_sums()
+        def tables():
+            landed(ids_in.at[: n_ea - 1], ids_r.at[0])
+            own_rows = jnp.concatenate([ids_in[o, 0] for o in range(n_ea)], axis=0)
+            own_columns = jnp.transpose(
+                jnp.concatenate(
+                    [own_rows.astype(F32), jnp.zeros((cap - n_ea, cap), F32)], axis=0
+                )
+            ).astype(jnp.int32)
+            for o in range(n_ea):
+                nodes_t[:, slabs(o)] = jnp.where(
+                    iota((enb, cap), 0) == ids_in[o, 0], 1.0, 0.0
+                ).astype(BF16)
+            for a in range(n_ea):
+                for b in range(n_ea):
+                    overlap[slabs(a), slabs(b)] = jnp.where(
+                        own_columns[:, a : a + 1] == own_rows[b : b + 1, :], 1.0, 0.0
+                    ).astype(BF16)
+
+        def layers():
+            yz_wait(0)
+            yz_apply(0)
+
+        orders = {1: (tables, first_sums, layers), n_ea - 1: (layers, tables, first_sums)}
+        usual = ek >= 0
+        for place, order in orders.items():
+            usual = jnp.logical_and(usual, ek != place)
+
+            @pl.when(ek == place)
+            def _():
+                for step in order:
+                    step()
+
+        @pl.when(usual)
+        def _():
+            tables()
+            layers()
+            first_sums()
+
         cells_step(0)
         x_wait(0)
         x_apply(0)
         if not wide:
             pl.semaphore_wait(known.at[1], expected)
         xy_send(1)
-        for a in range(n_ea):
-            for b in range(n_ea):
-                overlap[slabs(a), slabs(b)] = jnp.where(
-                    own_columns[:, a : a + 1] == own_rows[b : b + 1, :], 1.0, 0.0
-                ).astype(BF16)
         values = at_slots(1)
         landed(coup_in.at[: n_ea - 1], coup_r.at[0])
         for o in range(n_ea):

time: 20.4 us -> 20.5 us (level)
  no operation moved by 1% of the time
where the time goes in v11:
time: 20.5 us; the launch traced here: 20.3 us
  Pallas kernels  19.6 us (96%)
  between operations  0.64 us (3%)
    pallas_call x1, Pallas kernels, body(): pl.pallas_call(functools.partial(kernel, sizes, groups), out_shape=(pltpu...  18.9 us
    pallas_call x1, Pallas kernels, body(): pl.pallas_call(combine_kernel, out_shape=tuple((jax.ShapeDtypeStruct(like...  0.71 us

profile of v11, /device:TPU:0, one launch (start us, length us, event | category | flops | bytes accessed | tf_op | source)
XLA Modules:
  0.0 20.3 jit_solution(15655325290311706875)
XLA Ops:
  0.6 18.9 %krylov.1 = (f32[4,3,4,16,128]{4,3,2,1,0:T(8,128)S(1)}, f32[4,16,256]{2,1,0:T(8,128)S(1)}, f32[8,128]{1,0:T(8,128)S(1)}) custom-call(f32[3,4,16,128]{3,2,1,0:T(8,128)} %load_v.1, f32[15,256]{1,0:T(8,128)} %load_w.1, f32[4,16,128]{2,1,0:T(8,128)} %shift_h.1, f32[15,256]{1,0:T(8,128)} %diag_h.1, f32[15,15,256]{2,1,0:T(8,128)} %off_h.1, ...), custom_call_target="tpu_custom_call" | custom-call | tf_op jit(solution)/shard_map/krylov/pallas_call | solution.py:730
  19.6 0.7 %combine.1 = (f32[3,4,16,128]{3,2,1,0:T(8,128)}, f32[3,4,16,128]{3,2,1,0:T(8,128)}, f32[15,256]{1,0:T(8,128)}, f32[15,256]{1,0:T(8,128)}) custom-call(f32[4,3,4,16,128]{4,3,2,1,0:T(8,128)S(1)} %get-tuple-element.7.vu, f32[4,16,256]{2,1,0:T(8,128)S(1)} %get-tuple-element.8.wu, f32[8,128]{1,0:T(8,128)S(1)} %get-tuple-element.9.coefs), custom_call_target="tpu_custom_call" | custom-call | tf_op jit(solution)/shard_map/combine/pallas_call | solution.py:746

commit v12 on v11

--- a/solution.py
+++ b/solution.py
@@ -65,7 +65,7 @@
     load_v, load_w, shift_h, diag_h, off_h, coupling_h, kind_h, cell_h, node_h,
     vu, wu, coefs,
     w_first, shift, diag, off, coupling, cell, ids,
-    weights, win, stiff, lanes, rows, rows_b, nodes_mine, nodes_t, overlap,
+    weights, win, stiff, lanes, rows, rows_b, nodes_mine, nodes_t, overlap, turned,
     centre_diag, ids_in, coup_in,
     x_in, y_in, z_in, w_in, p_in, s_in, z_out, p_out, s_out, red, red_out,
     red_s, red_r,
@@ -513,10 +513,12 @@
             greet(known.at[1])
         ids_in[ek] = ids[:, 0, pl.ds(ek, 1), :]
         coup_in[ek] = coupling[:, :, block(0)]
+        late = ek == n_ea // 2
+
         def tables():
             landed(ids_in.at[: n_ea - 1], ids_r.at[0])
             own_rows = jnp.concatenate([ids_in[o, 0] for o in range(n_ea)], axis=0)
-            own_columns = jnp.transpose(
+            turned[...] = jnp.transpose(
                 jnp.concatenate(
                     [own_rows.astype(F32), jnp.zeros((cap - n_ea, cap), F32)], axis=0
                 )
@@ -525,52 +527,65 @@
                 nodes_t[:, slabs(o)] = jnp.where(
                     iota((enb, cap), 0) == ids_in[o, 0], 1.0, 0.0
                 ).astype(BF16)
+
+        def layers():
+            yz_wait(0)
+            yz_apply(0)
+
+        def finish_first():
+            cells_step(0)
+            x_wait(0)
+            x_apply(0)
+            xy_send(1)
+
+        def sums_first():
+            own_rows = jnp.concatenate([ids_in[o, 0] for o in range(n_ea)], axis=0)
+            own_columns = turned[...]
             for a in range(n_ea):
                 for b in range(n_ea):
                     overlap[slabs(a), slabs(b)] = jnp.where(
                         own_columns[:, a : a + 1] == own_rows[b : b + 1, :], 1.0, 0.0
                     ).astype(BF16)
-
-        def layers():
-            yz_wait(0)
-            yz_apply(0)
-
-        orders = {1: (tables, first_sums, layers), n_ea - 1: (layers, tables, first_sums)}
-        usual = ek >= 0
-        for place, order in orders.items():
-            usual = jnp.logical_and(usual, ek != place)
-
-            @pl.when(ek == place)
-            def _():
-                for step in order:
-                    step()
-
-        @pl.when(usual)
+            values = at_slots(1)
+            landed(coup_in.at[: n_ea - 1], coup_r.at[0])
+            for o in range(n_ea):
+                for i in range(comps):
+                    win[o, i] = masked(coup_in[o, i], ids_in[o, 1])
+            picks_wait(0)
+            terms = slot_terms(0)
+            values = values + folded(
+                jnp.dot(terms, overlap[...], preferred_element_type=F32)
+            )
+            sums_send(1, values)
+
+        @pl.when(ek == 1)
         def _():
             tables()
+            first_sums()
             layers()
+
+        @pl.when(ek != 1)
+        def _():
+            layers()
+            tables()
             first_sums()
 
-        cells_step(0)
-        x_wait(0)
-        x_apply(0)
         if not wide:
             pl.semaphore_wait(known.at[1], expected)
-        xy_send(1)
-        values = at_slots(1)
-        landed(coup_in.at[: n_ea - 1], coup_r.at[0])
-        for o in range(n_ea):
-            for i in range(comps):
-                win[o, i] = masked(coup_in[o, i], ids_in[o, 1])
-        picks_wait(0)
-        terms = slot_terms(0)
-        values = values + folded(
-            jnp.dot(terms, overlap[...], preferred_element_type=F32)
-        )
-        sums_send(1, values)
+
+        @pl.when(late)
+        def _():
+            sums_first()
+            finish_first()
+
+        @pl.when(jnp.logical_not(late))
+        def _():
+            finish_first()
+            sums_first()
+
         z_send(1)
         pick_send(1, pick(1))
-        nodes_step(0, terms)
+        nodes_step(0, slot_terms(0))
         for op in range(1, last):
             local(op)
             local_nodes(op)
@@ -580,8 +595,6 @@
             yz_apply(op)
             x_wait(op)
             x_apply(op)
-            late = ek == n_ea // 2
-
             @pl.when(late)
             def _():
                 sums_wait(op)
@@ -711,6 +724,7 @@
         vmem((n_ea, enb, cap), BF16),
         vmem((enb, slots), BF16),
         vmem((slots, slots), BF16),
+        vmem((cap, cap), jnp.int32),
         vmem((dx, dy, dz), F32),
         vmem((n_ea, 2, 1, cap), jnp.int32),
         vmem((n_ea, comps, ecomp, cap), F32),

time: 20.5 us -> 20.6 us (level)
  no operation moved by 1% of the time
where the time goes in v12:
time: 20.6 us; the launch traced here: 20.4 us
  Pallas kernels  19.7 us (96%)
  between operations  0.64 us (3%)
    pallas_call x1, Pallas kernels, body(): pl.pallas_call(functools.partial(kernel, sizes, groups), out_shape=(pltpu...  19 us
    pallas_call x1, Pallas kernels, body(): pl.pallas_call(combine_kernel, out_shape=tuple((jax.ShapeDtypeStruct(like...  0.71 us

profile of v12, /device:TPU:0, one launch (start us, length us, event | category | flops | bytes accessed | tf_op | source)
XLA Modules:
  0.0 20.4 jit_solution(16856514382096460960)
XLA Ops:
  0.6 19.0 %krylov.1 = (f32[4,3,4,16,128]{4,3,2,1,0:T(8,128)S(1)}, f32[4,16,256]{2,1,0:T(8,128)S(1)}, f32[8,128]{1,0:T(8,128)S(1)}) custom-call(f32[3,4,16,128]{3,2,1,0:T(8,128)} %load_v.1, f32[15,256]{1,0:T(8,128)} %load_w.1, f32[4,16,128]{2,1,0:T(8,128)} %shift_h.1, f32[15,256]{1,0:T(8,128)} %diag_h.1, f32[15,15,256]{2,1,0:T(8,128)} %off_h.1, ...), custom_call_target="tpu_custom_call" | custom-call | tf_op jit(solution)/shard_map/krylov/pallas_call | solution.py:744
  19.7 0.7 %combine.1 = (f32[3,4,16,128]{3,2,1,0:T(8,128)}, f32[3,4,16,128]{3,2,1,0:T(8,128)}, f32[15,256]{1,0:T(8,128)}, f32[15,256]{1,0:T(8,128)}) custom-call(f32[4,3,4,16,128]{4,3,2,1,0:T(8,128)S(1)} %get-tuple-element.7.vu, f32[4,16,256]{2,1,0:T(8,128)S(1)} %get-tuple-element.8.wu, f32[8,128]{1,0:T(8,128)S(1)} %get-tuple-element.9.coefs), custom_call_target="tpu_custom_call" | custom-call | tf_op jit(solution)/shard_map/combine/pallas_call | solution.py:760

commit v13 on v10

--- a/solution.py
+++ b/solution.py
@@ -40,23 +40,38 @@
     )
 
 
-def galerkin_coefficients(moment):
-    h = [moment[k + 1] + CENTRE * moment[k] for k in range(2 * ITERS - 1)]
-    first = 1.0 / h[0]
-    l1, l2 = h[1] * first, h[2] * first
-    d1 = h[2] - l1 * h[1]
-    e = h[3] - l1 * h[2]
-    g1 = moment[1] - l1 * moment[0]
-    second = 1.0 / d1
-    k = e * second
-    d2 = h[4] - l2 * h[2] - k * e
-    y2 = (moment[2] - l2 * moment[0] - k * g1) / d2
-    y1 = (g1 - e * y2) * second
-    y0 = (moment[0] - h[1] * y1 - h[2] * y2) * first
-    solution = [y0, y1, y2]
-    residual = [
-        1.0 - CENTRE * y0, -(y0 + CENTRE * y1), -(y1 + CENTRE * y2), -y2
-    ]
+def cg_coefficients(moment):
+    def inner(first, second):
+        total = None
+        for i, a in enumerate(first):
+            for j, b in enumerate(second):
+                term = a * b * moment[i + j]
+                total = term if total is None else total + term
+        return total
+
+    one = jnp.ones_like(moment[0])
+    residual, direction, solution = [one], [one], []
+    norm = moment[0]
+    for step in range(ITERS):
+        image = [CENTRE * d for d in direction] + [0.0 * one]
+        for i, d in enumerate(direction):
+            image[i + 1] = image[i + 1] + d
+        alpha = norm / inner(direction, image)
+        solution = [
+            (solution[i] if i < len(solution) else 0.0) + alpha * d
+            for i, d in enumerate(direction)
+        ]
+        residual = [
+            (residual[i] if i < len(residual) else 0.0) - alpha * d for i, d in enumerate(image)
+        ]
+        if step + 1 < ITERS:
+            new = inner(residual, residual)
+            ratio = new / norm
+            norm = new
+            direction = [
+                r + (ratio * direction[i] if i < len(direction) else 0.0)
+                for i, r in enumerate(residual)
+            ]
     return solution, residual
 
 
@@ -591,7 +606,6 @@
         packed = jnp.zeros((1, dz), F32)
         for n, m in enumerate(moments):
             packed = jnp.where(lane_r == n, jnp.sum(m, axis=1, keepdims=True), packed)
-        red_out[0, 0:1, :] = packed
         halos = (("ea", z_in, z_r), ("gy", y_in, y_r), ("gx", x_in, x_r))
         picks_wait(last)
         row = row + 2.0 * slot_moment(last)
@@ -599,7 +613,8 @@
             side_wait(name, buffer, sem, -1)
         row = row - 2.0 * near_moment(last)
         side_wait(*halos[2], -1)
-        red_out[0, 1:2, :] = row - 2.0 * far_moment(last)
+        final = jnp.sum(row - 2.0 * far_moment(last), axis=1, keepdims=True)
+        red_out[0] = jnp.where(lane_r == 2 * ITERS - 1, final, packed)
 
         red_start(0, groups[0])
         nodes_step(last, slot_terms(last))
@@ -633,9 +648,8 @@
         landed(red.at[stage, : total - 1], red_r.at[stage])
         reduced = jnp.sum(red[stage, :total], axis=0)
 
-    early = [jnp.broadcast_to(reduced[0:1, n : n + 1], (1, dz)) for n in range(2 * ITERS - 1)]
-    final = jnp.broadcast_to(jnp.sum(reduced[1:2], axis=1, keepdims=True), (1, dz))
-    sol, res = galerkin_coefficients(early + [final])
+    early = [jnp.broadcast_to(reduced[:, n : n + 1], (1, dz)) for n in range(2 * ITERS)]
+    sol, res = cg_coefficients(early)
     for n, c in enumerate(sol + res):
         coefs[n : n + 1, :] = c
 
@@ -704,8 +718,8 @@
         vmem((ITERS, 2, 8, dz), F32),
         vmem((ITERS, n_ea, comps, cap), F32),
         vmem((ITERS, n_ea, comps, cap), F32),
-        vmem((len(groups), widest, 2, dz), F32),
-        vmem((len(groups), 2, dz), F32),
+        vmem((len(groups), widest, 1, dz), F32),
+        vmem((len(groups), 1, dz), F32),
         dma((len(groups),)), dma((len(groups),)),
     ]
     basis = pl.pallas_call(

time: 20.4 us -> 20.5 us (level)
  no operation moved by 1% of the time
where the time goes in v13:
time: 20.5 us; the launch traced here: 20.2 us
  Pallas kernels  19.6 us (96%)
  between operations  0.64 us (3%)
    pallas_call x1, Pallas kernels, body(): pl.pallas_call(functools.partial(kernel, sizes, groups), out_shape=(pltpu...  18.9 us
    pallas_call x1, Pallas kernels, body(): pl.pallas_call(combine_kernel, out_shape=tuple((jax.ShapeDtypeStruct(like...  0.71 us

profile of v13, /device:TPU:0, one launch (start us, length us, event | category | flops | bytes accessed | tf_op | source)
XLA Modules:
  0.0 20.2 jit_solution(13219686441435097601)
XLA Ops:
  0.6 18.9 %krylov.1 = (f32[4,3,4,16,128]{4,3,2,1,0:T(8,128)S(1)}, f32[4,16,256]{2,1,0:T(8,128)S(1)}, f32[8,128]{1,0:T(8,128)S(1)}) custom-call(f32[3,4,16,128]{3,2,1,0:T(8,128)} %load_v.1, f32[15,256]{1,0:T(8,128)} %load_w.1, f32[4,16,128]{2,1,0:T(8,128)} %shift_h.1, f32[15,256]{1,0:T(8,128)} %diag_h.1, f32[15,15,256]{2,1,0:T(8,128)} %off_h.1, ...), custom_call_target="tpu_custom_call" | custom-call | tf_op jit(solution)/shard_map/krylov/pallas_call | solution.py:725
  19.5 0.7 %combine.1 = (f32[3,4,16,128]{3,2,1,0:T(8,128)}, f32[3,4,16,128]{3,2,1,0:T(8,128)}, f32[15,256]{1,0:T(8,128)}, f32[15,256]{1,0:T(8,128)}) custom-call(f32[4,3,4,16,128]{4,3,2,1,0:T(8,128)S(1)} %get-tuple-element.7.vu, f32[4,16,256]{2,1,0:T(8,128)S(1)} %get-tuple-element.8.wu, f32[8,128]{1,0:T(8,128)S(1)} %get-tuple-element.9.coefs), custom_call_target="tpu_custom_call" | custom-call | tf_op jit(solution)/shard_map/combine/pallas_call | solution.py:741
